TPU v7x, 512 devices: a whole 4x8x8 slice. The times are simulated.
512 devices in a mesh: row: 32 (over x, y), shift: 16 (over z, core).
Axes of the slice: x: 4, y: 8, z: 8, core: 2. Of those that a mesh axis runs over, the one named last changes fastest.
Arguments:
- snapshots: bfloat16 [4096, 2, 128], P('row'), may hold values from -6 to 6
- tail_sensors: bfloat16 [128, 2, 128], replicated, may hold values from -6 to 6
- shift_offsets: int32 [48], P('shift'), may hold values from 0 to 128
- start_basis: float32 [64, 4096], P(None, 'row'), may hold values from -0.09375 to 0.09375
Outputs:
- covariance: float32 [4096, 4096], P('row', 'shift')
- signal_basis: float32 [64, 4096], P(None, 'row')
Inputs may be any that keep to these rules, and one draw needn't show every extreme that they name: `shift_offsets`: each shift's first sensor.
All inputs are finite; a program needn't handle non-finite values.
Results may differ from a plain program's by a relative error of at most 0.0031.
Values may be sent and summed in bfloat16 or wider, within the bound.
No kernel may reach another device: no remote copies, remote signals or barrier semaphores. Data moves between devices by JAX's collectives and lax.ppermute only.
A program may use at most 64 MiB of HBM per device.

v0:
```python
import jax
import jax.numpy as jnp
from jax import lax
from jax.experimental import pallas as pl
from jax.experimental.pallas import tpu as pltpu
from jax.sharding import Mesh
from jax.sharding import PartitionSpec as P


K = 64
SNAPS = 128
SHIFTS = 48
BLOCK = 128
GROUP = 2
ROW = ("row_0", "row_1")
SHIFT = ("z", "core")
EVERY = (*ROW, *SHIFT)
HALF_ROOT = 0.7071067811865476
HIGH = lax.Precision.HIGHEST


def dot_nt(a, b, precision=None):
    return lax.dot_general(
        a, b, (((1,), (1,)), ((), ())), precision=precision, preferred_element_type=jnp.float32
    )


def dot_nn(a, b, precision=None):
    return lax.dot_general(
        a, b, (((1,), (0,)), ((), ())), precision=precision, preferred_element_type=jnp.float32
    )


def sent_to_all(x, axis):
    copies = jnp.broadcast_to(x, (lax.axis_size(axis), *x.shape))
    return lax.all_to_all(copies, axis, split_axis=0, concat_axis=0, tiled=True)


def covariance_kernel(
    place, offsets, own, after, mirror, mirror_after, tail, pieces, basis,
    cov, mapped, row_w, row_z, col_w, col_z, acc,
):
    r = place[0]
    c = place[1]
    flip = (
        lax.broadcasted_iota(jnp.int32, (BLOCK, BLOCK), 0)
        + lax.broadcasted_iota(jnp.int32, (BLOCK, BLOCK), 1)
        == BLOCK - 1
    ).astype(jnp.bfloat16)

    def put_window(ref, at, block, upper):
        re = block[:, :SNAPS].astype(jnp.float32) * HALF_ROOT
        im = block[:, SNAPS:].astype(jnp.float32) * HALF_ROOT
        ref[0, pl.ds(at, BLOCK), :] = jnp.where(upper, re, im)
        ref[1, pl.ds(at, BLOCK), :] = jnp.where(upper, im, -re)

    def put_mirror(ref, at, block, upper):
        turned = dot_nn(flip, block) * HALF_ROOT
        re = turned[:, :SNAPS]
        im = turned[:, SNAPS:]
        ref[0, pl.ds(at, BLOCK), :] = jnp.where(upper, re, -im)
        ref[1, pl.ds(at, BLOCK), :] = jnp.where(upper, im, re)

    row_upper = r < 16
    put_window(row_w, 0, own[...], row_upper)
    put_window(row_w, BLOCK, jnp.where(r == 31, tail[...], after[...]), row_upper)
    put_mirror(row_z, 0, jnp.where(r == 0, tail[...], mirror_after[...]), row_upper)
    put_mirror(row_z, BLOCK, mirror[...], row_upper)

    odd = [jnp.concatenate([pieces[2 * i + j, :16, :] for i in range(8)], axis=0) for j in range(2)]
    even = [jnp.concatenate([pieces[16 + 4 * i + j] for i in range(4)], axis=0) for j in range(4)]
    col_upper = c < 8
    put_window(col_w, 0, even[0], col_upper)
    put_window(col_w, BLOCK, odd[0], col_upper)
    put_window(col_w, 2 * BLOCK, jnp.where(c == 15, tail[...], even[2]), col_upper)
    put_mirror(col_z, 0, jnp.where(c == 0, tail[...], even[3]), col_upper)
    put_mirror(col_z, BLOCK, odd[1], col_upper)
    put_mirror(col_z, 2 * BLOCK, even[1], col_upper)

    acc[...] = jnp.zeros(acc.shape, jnp.float32)

    def step(at, carry):
        left, right = [], []
        for u in range(3 * GROUP):
            o = offsets[at * GROUP + u // 3, u % 3]
            for plane in range(2):
                left.append(
                    (row_w[plane, pl.ds(o, BLOCK), :] + row_z[plane, pl.ds(BLOCK - o, BLOCK), :])
                    .astype(jnp.bfloat16)
                )
                right.append(
                    (col_w[plane, pl.ds(o, 2 * BLOCK), :] + col_z[plane, pl.ds(BLOCK - o, 2 * BLOCK), :])
                    .astype(jnp.bfloat16)
                )
        acc[...] += dot_nt(jnp.concatenate(left, axis=1), jnp.concatenate(right, axis=1))
        return carry

    lax.fori_loop(0, 16 // GROUP, step, 0)
    block = acc[...] * (1.0 / (SNAPS * SHIFTS))
    cov[...] = block
    image = dot_nn(basis[...], block, HIGH)
    for p in range(32):
        mapped[p] = image[4 * (p // 2) : 4 * (p // 2) + 4, SNAPS * (p % 2) : SNAPS * (p % 2) + SNAPS]


def covariance_block(place, offsets, own, after, mirror, mirror_after, tail, pieces, basis):
    vmem = pl.BlockSpec(memory_space=pltpu.VMEM)
    return pl.pallas_call(
        covariance_kernel,
        name="covariance_block",
        in_specs=[pl.BlockSpec(memory_space=pltpu.SMEM)] * 2 + [vmem] * 7,
        out_specs=[vmem, vmem],
        out_shape=[
            jax.ShapeDtypeStruct((BLOCK, 2 * BLOCK), jnp.float32),
            jax.ShapeDtypeStruct((32, 4, SNAPS), jnp.float32),
        ],
        scratch_shapes=[
            pltpu.VMEM((2, 2 * BLOCK, SNAPS), jnp.float32),
            pltpu.VMEM((2, 2 * BLOCK, SNAPS), jnp.float32),
            pltpu.VMEM((2, 3 * BLOCK, SNAPS), jnp.float32),
            pltpu.VMEM((2, 3 * BLOCK, SNAPS), jnp.float32),
            pltpu.VMEM((BLOCK, 2 * BLOCK), jnp.float32),
        ],
    )(place, offsets, own, after, mirror, mirror_after, tail, pieces, basis)


def inverse_factor(gram):
    row_at = lax.broadcasted_iota(jnp.int32, (8, 2 * K), 0)
    lane_at = lax.broadcasted_iota(jnp.int32, (8, 2 * K), 1)
    tiles, done = [], []
    for t in range(K // 8):
        part = gram[8 * t : 8 * t + 8]
        eye = (lane_at == row_at + (K + 8 * t)).astype(jnp.float32)
        tiles.append(jnp.where(lane_at < K, jnp.concatenate([part, part], axis=1), eye))
        done.append(jnp.zeros((8, 2 * K), jnp.float32))
    for at in range(K // 8):
        own, rest = at, range(at + 1, K // 8)
        cols = [
            [jnp.broadcast_to(tiles[t][:, j : j + 1], (8, 2 * K)) for t in range(at, K // 8)]
            for j in range(8 * at, 8 * at + 8)
        ]
        for s in range(8):
            col = cols[s]
            below = row_at > s
            pivot = col[0][s : s + 1, :]
            inverse = 1.0 / pivot
            row = tiles[own][s : s + 1, :]
            scaled = row * inverse
            done[own] = jnp.where(row_at == s, row / jnp.sqrt(pivot), done[own])
            for k in range(s + 1, 8):
                share = cols[k][0][s : s + 1, :] * inverse
                left = [c - f * share for c, f in zip(cols[k], col)]
                left[0] = jnp.where(below, left[0], cols[k][0])
                cols[k] = left
            tiles[own] = jnp.where(below, tiles[own] - col[0] * scaled, tiles[own])
            for t in rest:
                tiles[t] = tiles[t] - col[t - at] * scaled
    return jnp.concatenate(done, axis=0)[:, K:]


def image_kernel(place, mapped, cov, kept, sent):
    image = jnp.concatenate(
        [jnp.concatenate([mapped[2 * i], mapped[2 * i + 1]], axis=1) for i in range(16)], axis=0
    )
    product = dot_nt(image, cov[...], HIGH)
    gram = dot_nt(image, image, HIGH)
    terms = jnp.concatenate([product, halves_side_by_side(gram)], axis=0)
    half = terms.shape[0] // 2
    first = place[1] % 2 == 0
    kept[...] = jnp.where(first, terms[:half], terms[half:])
    sent[...] = jnp.where(first, terms[half:], terms[:half])


def halves_side_by_side(gram):
    return jnp.concatenate([gram[: K // 2], gram[K // 2 :]], axis=1)


def halves_stacked(packed):
    return jnp.concatenate([packed[:, :K], packed[:, K:]], axis=0)


def first_factor_kernel(place, mine, other, mapped, grams):
    first = place[1] % 2 == 0
    total = jnp.concatenate(
        [jnp.where(first, mine[...], other[...]), jnp.where(first, other[...], mine[...])], axis=0
    )
    image = dot_nn(inverse_factor(halves_stacked(total[K:])), total[:K], HIGH)
    mapped[...] = image
    part = halves_side_by_side(dot_nt(image, image, HIGH))
    for i in range(grams.shape[0]):
        grams[i] = part


def last_factor_kernel(grams, mapped, basis):
    total = jnp.sum(grams[...], axis=0)
    basis[...] = dot_nn(inverse_factor(halves_stacked(total)), mapped[...], HIGH)


def local_call(kernel, shapes, *operands):
    spaces = [pltpu.SMEM if x.dtype == jnp.int32 else pltpu.VMEM for x in operands]
    return pl.pallas_call(
        kernel,
        in_specs=[pl.BlockSpec(memory_space=space) for space in spaces],
        out_shape=[jax.ShapeDtypeStruct(s, jnp.float32) for s in shapes],
    )(*operands)


def exchanged(tiles, axis):
    return lax.all_to_all(tiles, axis, split_axis=0, concat_axis=0, tiled=True)


def total_over(tiles, axis):
    return sent_to_all(exchanged(tiles, axis).sum(axis=0), axis)


def piece_routes():
    routes = []
    for b in range(32):
        for q in range(16):
            if b % 2:
                c = (b - 1) // 2 if q % 2 == 0 else (31 - b) // 2
                to = q
            else:
                c = (b // 2, (30 - b) // 2, (b // 2 - 1) % 16, (16 - b // 2) % 16)[q % 4]
                to = q + 16
            routes.append((b * 16 + q, to * 16 + c))
    return routes


def per_device(snapshots, tail_sensors, shift_offsets, start_basis):
    r = lax.axis_index(ROW)
    c = lax.axis_index(SHIFT)
    own = snapshots.reshape(BLOCK, 2 * SNAPS)
    tail = tail_sensors.reshape(BLOCK, 2 * SNAPS)
    offsets = jnp.zeros((16, 2 * SNAPS), jnp.bfloat16)
    offsets = lax.dynamic_update_slice(offsets, shift_offsets.astype(jnp.bfloat16)[None], (0, 0))
    odd_piece = jnp.concatenate([lax.dynamic_slice_in_dim(own, 16 * (c // 2), 16, 0), offsets], 0)
    even_piece = lax.dynamic_slice_in_dim(own, 32 * (c // 4), 32, 0)
    piece = jnp.where(r % 2 == 1, odd_piece, even_piece)
    piece = lax.ppermute(piece, EVERY, piece_routes())
    after = lax.ppermute(own, ROW, [(i, (i - 1) % 32) for i in range(32)])
    mirror = lax.ppermute(own, ROW, [(i, 31 - i) for i in range(32)])
    mirror_after = lax.ppermute(own, ROW, [(i, (32 - i) % 32) for i in range(32)])
    pieces = sent_to_all(piece, "row_1")
    pieces = sent_to_all(pieces, "row_0").reshape(32, 32, 2 * SNAPS)
    every_offset = pieces[:16, 16, :3].astype(jnp.int32)
    place = jnp.stack([r, c]).astype(jnp.int32)
    cov, mapped = covariance_block(
        place, every_offset, own, after, mirror, mirror_after, tail, pieces, start_basis
    )
    mapped = total_over(mapped, ROW)
    half = (3 * K // 4, BLOCK)
    kept, sent = local_call(image_kernel, [half, half], place, mapped, cov)
    swap = [(0, 1), (1, 0)]
    mine = sent_to_all(kept + lax.ppermute(sent, "core", swap), "z").sum(axis=0)
    other = lax.ppermute(mine, "core", swap)
    mapped, grams = local_call(
        first_factor_kernel, [(K, BLOCK), (4, K // 2, 2 * K)], place, mine, other
    )
    grams = sent_to_all(exchanged(grams, "row_0").sum(axis=0), "row_1")
    (basis,) = local_call(last_factor_kernel, [(K, BLOCK)], grams, mapped)
    return (cov, basis)


def solution(mesh):
    split = Mesh(mesh.devices.reshape(4, 8, 8, 2), EVERY)
    in_specs = (P(ROW, None, None), P(), P(SHIFT), P(None, ROW))
    out_specs = (P(ROW, SHIFT), P(None, ROW))
    return jax.shard_map(
        per_device, mesh=split, in_specs=in_specs, out_specs=out_specs, check_vma=False
    )
```

profile of v0, /device:TPU:1, one launch (start us, length us, event | category | flops | bytes accessed | tf_op | source)
XLA Modules:
  0.0 152.3 jit_solution(2191457288711857140)
XLA Ops:
  0.6 0.0 copy-start.6
  0.7 0.0 copy-start.9
  0.7 0.6 copy-done.9
  1.3 0.1 copy-done.6
  1.5 0.0 copy-start.1
  1.6 15.0 %collective-permute-start = (bf16[32,256]{1,0:T(8,128)(2,1)S(1)}, bf16[32,256]{1,0:T(8,128)(2,1)S(1)}, u32[]{:S(2)}, u32[]{:S(2)}) collective-permute-start(bf16[32,256]{1,0:T(8,128)(2,1)S(1)} %fusion.2), channel_id=1, source_target_pairs={{0,256},{1,287},{2,303},{3,304},{4,320},{5,351},{6,367},{7,368},{8... | collective-permute-start | bytes 49160 | tf_op jit(solution)/shard_map/ppermute | solution.py:240
  16.5 0.8 collective-permute-done
  17.4 13.2 %all_to_all.35 = bf16[8,32,256]{2,1,0:T(8,128)(2,1)S(1)} all-to-all(bf16[8,32,256]{2,1,0:T(8,128)(2,1)S(1)} %broadcast_in_dim.20), channel_id=1, replica_groups=mesh['row_0'=4,'row_1'=8,'z'=8,'core'=2] {'row_1'}, dimensions={0} | all-to-all | bytes 262144 | tf_op jit(solution)/shard_map/all_to_all | solution.py:36
  30.6 0.9 broadcast_in_dim.21
  31.4 0.0 copy-start.7
  31.4 3.6 %all-to-all-start.1 = ((bf16[4,8,32,256]{3,2,1,0:T(8,128)(2,1)}), bf16[4,8,32,256]{3,2,1,0:T(8,128)(2,1)S(1)}, u32[]{:S(2)}, u32[]{:S(2)}) async-start(bf16[4,8,32,256]{3,2,1,0:T(8,128)(2,1)} %broadcast_in_dim.21), calls=%async_computation.1 | async-start | bytes 1048576 | tf_op jit(solution)/shard_map/all_to_all | solution.py:36
  35.0 4.1 %collective-permute-start.1 = (bf16[128,256]{1,0:T(8,128)(2,1)S(1)}, bf16[128,256]{1,0:T(8,128)(2,1)S(1)}, u32[]{:S(2)}, u32[]{:S(2)}) collective-permute-start(bf16[128,256]{1,0:T(8,128)(2,1)S(1)} %bitcast.18), channel_id=1, source_target_pairs={{0,496},{16,0},{32,16},{48,32},{64,48},{80,64},{96,80},{112,96},{1... | collective-permute-start | bytes 196616 | tf_op jit(solution)/shard_map/ppermute | solution.py:241
  39.2 2.4 %collective-permute-start.2 = (bf16[128,256]{1,0:T(8,128)(2,1)S(1)}, bf16[128,256]{1,0:T(8,128)(2,1)S(1)}, u32[]{:S(2)}, u32[]{:S(2)}) collective-permute-start(bf16[128,256]{1,0:T(8,128)(2,1)S(1)} %bitcast.19), channel_id=1, source_target_pairs={{0,496},{16,480},{32,464},{48,448},{64,432},{80,416},{96,400},{112... | collective-permute-start | bytes 196616 | tf_op jit(solution)/shard_map/ppermute | solution.py:242
  41.6 0.0 copy-done.1
  41.6 0.7 collective-permute-start.3
  42.3 0.0 copy-done.7
  42.3 0.6 copy.17
  42.9 0.7 pad_add_fusion.place
  43.6 0.0 all-to-all-done.1
  43.6 0.0 copy-start
  43.6 0.7 slice_convert_fusion
  44.3 0.0 collective-permute-done.1.after
  44.3 0.0 copy-start.3
  44.3 3.8 %collective-permute-done.2.mirror = bf16[128,256]{1,0:T(8,128)(2,1)S(1)} collective-permute-done((bf16[128,256]{1,0:T(8,128)(2,1)S(1)}, bf16[128,256]{1,0:T(8,128)(2,1)S(1)}, u32[]{:S(2)}, u32[]{:S(2)}) %collective-permute-start.2) | collective-permute-done | bytes 65568 | tf_op jit(solution)/shard_map/ppermute | solution.py:242
  48.1 0.0 copy-start.4
  48.1 0.0 collective-permute-done.3.mirror_after
  48.1 0.0 copy-start.5
  48.1 0.0 copy-done
  48.1 0.0 copy-done.3
  48.1 0.6 copy-done.4
  48.7 0.0 copy-done.5
  48.7 6.6 %covariance_block.1 = (f32[128,256]{1,0:T(8,128)}, f32[32,4,128]{2,1,0:T(4,128)}) custom-call(s32[2]{0:T(128)} %pad_add_fusion.place, s32[16,3]{1,0:T(8,128)} %bitcast.25, bf16[128,256]{1,0:T(8,128)(2,1)} %bitcast.21, bf16[128,256]{1,0:T(8,128)(2,1)} %copy-done.3, bf16[128,256]{1,0:T(8,128)(2,1)} %copy-done.4, bf16[128,256]{1,0:T(8,128)(2,1)} %copy-done.5, ...), custom_call_target="tpu_custom_call" | custom-call | tf_op jit(solution)/shard_map/covariance_block/pallas_call | solution.py:108
  55.3 19.4 %all_to_all.36 = f32[32,4,128]{2,1,0:T(4,128)S(1)} all-to-all(f32[32,4,128]{2,1,0:T(4,128)} %get-tuple-element.9), channel_id=1, replica_groups=mesh['row_0'=4,'row_1'=8,'z'=8,'core'=2] {'row_0','row_1'}, dimensions={0} | all-to-all | bytes 131072 | tf_op jit(solution)/shard_map/all_to_all | solution.py:209
  74.8 12.5 %all_to_all.37.mapped = f32[32,4,128]{2,1,0:T(4,128)} all-to-all(f32[32,4,128]{2,1,0:T(4,128)S(1)} %broadcast_in_dim.22), channel_id=1, replica_groups=mesh['row_0'=4,'row_1'=8,'z'=8,'core'=2] {'row_0','row_1'}, dimensions={0} | all-to-all | bytes 131072 | tf_op jit(solution)/shard_map/all_to_all | solution.py:36
  87.3 1.9 %shard_map.59 = (f32[48,128]{1,0:T(8,128)}, f32[48,128]{1,0:T(8,128)}) custom-call(s32[2]{0:T(128)} %pad_add_fusion.place, f32[32,4,128]{2,1,0:T(4,128)} %all_to_all.37.mapped, f32[128,256]{1,0:T(8,128)} %get-tuple-element.6.cov), custom_call_target="tpu_custom_call" | custom-call | tf_op jit(solution)/shard_map/pallas_call | solution.py:201
  89.2 10.2 %collective-permute-start.4 = (f32[48,128]{1,0:T(8,128)}, f32[48,128]{1,0:T(8,128)S(1)}, u32[]{:S(2)}, u32[]{:S(2)}) collective-permute-start(f32[48,128]{1,0:T(8,128)} %get-tuple-element.11), channel_id=1, source_target_pairs={{0,1},{1,0},{2,3},{3,2},{4,5},{5,4},{6,7},{7,6},{8,9},{9,8},{10,11... | collective-permute-start | bytes 73736 | tf_op jit(solution)/shard_map/ppermute | solution.py:255
  99.4 1.0 collective-permute-done.4
  100.4 0.7 add.28
  101.2 20.1 %all_to_all.38 = f32[8,48,128]{2,1,0:T(8,128)S(1)} all-to-all(f32[8,48,128]{2,1,0:T(8,128)S(1)} %broadcast_in_dim.23), channel_id=1, replica_groups=mesh['row_0'=4,'row_1'=8,'z'=8,'core'=2] {'z'}, dimensions={0} | all-to-all | bytes 393216 | tf_op jit(solution)/shard_map/all_to_all | solution.py:36
  121.4 0.0 copy-start.2
  121.4 3.9 %collective-permute-start.5 = (f32[48,128]{1,0:T(8,128)S(1)}, f32[48,128]{1,0:T(8,128)S(1)}, u32[]{:S(2)}, u32[]{:S(2)}) collective-permute-start(f32[48,128]{1,0:T(8,128)S(1)} %reduce_sum.28.mine), channel_id=1, source_target_pairs={{0,1},{1,0},{2,3},{3,2},{4,5},{5,4},{6,7},{7,6},{8,9},{9,8},{10,11... | collective-permute-start | bytes 73736 | tf_op jit(solution)/shard_map/ppermute | solution.py:256
  125.3 0.8 collective-permute-done.5.other
  126.1 0.0 copy-done.2
  126.1 0.6 copy-done.8
  126.7 3.5 %shard_map.60 = (f32[64,128]{1,0:T(8,128)}, f32[4,32,128]{2,1,0:T(8,128)}) custom-call(s32[2]{0:T(128)} %pad_add_fusion.place, f32[48,128]{1,0:T(8,128)} %copy-done.2, f32[48,128]{1,0:T(8,128)} %copy-done.8), custom_call_target="tpu_custom_call" | custom-call | tf_op jit(solution)/shard_map/pallas_call | solution.py:201
  130.2 7.7 %all_to_all.39 = f32[4,32,128]{2,1,0:T(8,128)S(1)} all-to-all(f32[4,32,128]{2,1,0:T(8,128)} %get-tuple-element.12), channel_id=1, replica_groups=mesh['row_0'=4,'row_1'=8,'z'=8,'core'=2] {'row_0'}, dimensions={0} | all-to-all | bytes 131072 | tf_op jit(solution)/shard_map/all_to_all | solution.py:209
  138.0 11.0 %all_to_all.40.grams = f32[8,32,128]{2,1,0:T(8,128)} all-to-all(f32[8,32,128]{2,1,0:T(8,128)S(1)} %broadcast_in_dim.24), channel_id=1, replica_groups=mesh['row_0'=4,'row_1'=8,'z'=8,'core'=2] {'row_1'}, dimensions={0} | all-to-all | bytes 262144 | tf_op jit(solution)/shard_map/all_to_all | solution.py:36
  149.0 3.3 %shard_map.61 = f32[64,128]{1,0:T(8,128)} custom-call(f32[8,32,128]{2,1,0:T(8,128)} %all_to_all.40.grams, f32[64,128]{1,0:T(8,128)} %get-tuple-element.13.mapped), custom_call_target="tpu_custom_call" | custom-call | tf_op jit(solution)/shard_map/pallas_call | solution.py:201
  (12 shorter events, 0.2 us)
Async XLA Ops:
  0.6 0.8 copy-start.6
  0.7 0.7 copy-start.9
  1.5 40.1 %copy-start.1 = (bf16[16,8,2,128]{3,1,2,0:T(8,128)(2,1)}, bf16[16,8,2,128]{3,1,2,0:T(8,128)(2,1)S(1)}, u32[]{:S(2)}) copy-start(bf16[16,8,2,128]{3,1,2,0:T(8,128)(2,1)S(1)} %copy.18) | copy-start | bytes 196612
  1.6 15.8 %collective-permute-start = (bf16[32,256]{1,0:T(8,128)(2,1)S(1)}, bf16[32,256]{1,0:T(8,128)(2,1)S(1)}, u32[]{:S(2)}, u32[]{:S(2)}) collective-permute-start(bf16[32,256]{1,0:T(8,128)(2,1)S(1)} %fusion.2), channel_id=1, source_target_pairs={{0,256},{1,287},{2,303},{3,304},{4,320},{5,351},{6,367},{7,368},{8... | collective-permute-start | bytes 49160 | tf_op jit(solution)/shard_map/ppermute | solution.py:240
  31.4 10.9 %copy-start.7 = (bf16[128,2,128]{2,1,0:T(2,128)(2,1)S(1)}, bf16[128,2,128]{2,1,0:T(2,128)(2,1)}, u32[]{:S(2)}) copy-start(bf16[128,2,128]{2,1,0:T(2,128)(2,1)} %param.5) | copy-start | bytes 196612
  31.4 12.2 %all-to-all-start.1 = ((bf16[4,8,32,256]{3,2,1,0:T(8,128)(2,1)}), bf16[4,8,32,256]{3,2,1,0:T(8,128)(2,1)S(1)}, u32[]{:S(2)}, u32[]{:S(2)}) async-start(bf16[4,8,32,256]{3,2,1,0:T(8,128)(2,1)} %broadcast_in_dim.21), calls=%async_computation.1 | async-start | bytes 1048576 | tf_op jit(solution)/shard_map/all_to_all | solution.py:36
  35.0 9.2 %collective-permute-start.1 = (bf16[128,256]{1,0:T(8,128)(2,1)S(1)}, bf16[128,256]{1,0:T(8,128)(2,1)S(1)}, u32[]{:S(2)}, u32[]{:S(2)}) collective-permute-start(bf16[128,256]{1,0:T(8,128)(2,1)S(1)} %bitcast.18), channel_id=1, source_target_pairs={{0,496},{16,0},{32,16},{48,32},{64,48},{80,64},{96,80},{112,96},{1... | collective-permute-start | bytes 196616 | tf_op jit(solution)/shard_map/ppermute | solution.py:241
  39.2 8.9 %collective-permute-start.2 = (bf16[128,256]{1,0:T(8,128)(2,1)S(1)}, bf16[128,256]{1,0:T(8,128)(2,1)S(1)}, u32[]{:S(2)}, u32[]{:S(2)}) collective-permute-start(bf16[128,256]{1,0:T(8,128)(2,1)S(1)} %bitcast.19), channel_id=1, source_target_pairs={{0,496},{16,480},{32,464},{48,448},{64,432},{80,416},{96,400},{112... | collective-permute-start | bytes 196616 | tf_op jit(solution)/shard_map/ppermute | solution.py:242
  41.6 6.5 %collective-permute-start.3 = (bf16[128,256]{1,0:T(8,128)(2,1)S(1)}, bf16[128,256]{1,0:T(8,128)(2,1)S(1)}, u32[]{:S(2)}, u32[]{:S(2)}) collective-permute-start(bf16[128,256]{1,0:T(8,128)(2,1)S(1)} %bitcast.20), channel_id=1, source_target_pairs={{0,0},{16,496},{32,480},{48,464},{64,448},{80,432},{96,416},{112,4... | collective-permute-start | bytes 196616 | tf_op jit(solution)/shard_map/ppermute | solution.py:243
  43.6 4.5 %copy-start = (bf16[4,8,32,256]{3,2,1,0:T(8,128)(2,1)}, bf16[4,8,32,256]{3,2,1,0:T(8,128)(2,1)S(1)}, u32[]{:S(2)}) copy-start(bf16[4,8,32,256]{3,2,1,0:T(8,128)(2,1)S(1)} %all-to-all-done.1) | copy-start | bytes 1572868
  44.3 3.8 %copy-start.3 = (bf16[128,256]{1,0:T(8,128)(2,1)}, bf16[128,256]{1,0:T(8,128)(2,1)S(1)}, u32[]{:S(2)}) copy-start(bf16[128,256]{1,0:T(8,128)(2,1)S(1)} %collective-permute-done.1.after) | copy-start | bytes 196612
  48.1 0.6 copy-start.4
  48.1 0.7 copy-start.5
  89.2 11.2 %collective-permute-start.4 = (f32[48,128]{1,0:T(8,128)}, f32[48,128]{1,0:T(8,128)S(1)}, u32[]{:S(2)}, u32[]{:S(2)}) collective-permute-start(f32[48,128]{1,0:T(8,128)} %get-tuple-element.11), channel_id=1, source_target_pairs={{0,1},{1,0},{2,3},{3,2},{4,5},{5,4},{6,7},{7,6},{8,9},{9,8},{10,11... | collective-permute-start | bytes 73736 | tf_op jit(solution)/shard_map/ppermute | solution.py:255
  121.4 4.7 %copy-start.2 = (f32[48,128]{1,0:T(8,128)}, f32[48,128]{1,0:T(8,128)S(1)}, u32[]{:S(2)}) copy-start(f32[48,128]{1,0:T(8,128)S(1)} %reduce_sum.28.mine) | copy-start | bytes 73732
  121.4 4.7 %collective-permute-start.5 = (f32[48,128]{1,0:T(8,128)S(1)}, f32[48,128]{1,0:T(8,128)S(1)}, u32[]{:S(2)}, u32[]{:S(2)}) collective-permute-start(f32[48,128]{1,0:T(8,128)S(1)} %reduce_sum.28.mine), channel_id=1, source_target_pairs={{0,1},{1,0},{2,3},{3,2},{4,5},{5,4},{6,7},{7,6},{8,9},{9,8},{10,11... | collective-permute-start | bytes 73736 | tf_op jit(solution)/shard_map/ppermute | solution.py:256
  126.1 0.6 copy-start.8
where the time goes:
time: 153 us; the launch traced here: 152 us
  blocking collectives  84 us (55%)
  starting transfers between devices  39.8 us (26%)
  Pallas kernels  15.4 us (10%)
  waiting for transfers between devices  6.53 us (4%)
  local copies, waits for them, and re-layouts  3.62 us (2%)
  other arithmetic  2.13 us (1%)
    all_to_all x4, blocking collectives, sent_to_all(): return lax.all_to_all(copies, axis, split_axis=0, concat_axis=0, tiled=True)  56.8 us
    all_to_all x2, blocking collectives, exchanged(): return lax.all_to_all(tiles, axis, split_axis=0, concat_axis=0, tiled=True)  27.2 us
    ppermute x1, starting transfers between devices, per_device(): piece = lax.ppermute(piece, EVERY, piece_routes())  15 us
    ppermute x1, starting transfers between devices, per_device(): mine = sent_to_all(kept + lax.ppermute(sent, 'core', swap), 'z').sum(axis=0)  10.2 us
    pallas_call x3, Pallas kernels, local_call(): pl.pallas_call(kernel, in_specs=[pl.BlockSpec(memory_space=space) for spa...  8.77 us
    pallas_call x1, Pallas kernels, covariance_block(): pl.pallas_call(covariance_kernel, name='covariance_block', in_specs=[pl.B...  6.58 us
    ppermute x1, starting transfers between devices, per_device(): after = lax.ppermute(own, ROW, [(i, (i - 1) % 32) for i in range(32)])  4.13 us
    ppermute x1, starting transfers between devices, per_device(): other = lax.ppermute(mine, 'core', swap)  3.87 us
  transfers between devices with their start and end apart: 7, of which 4 were waited for; matrix products, arithmetic and copies ran while one was open for 1% of the time, Pallas kernels for 0%

commit v1 on v0

--- a/solution.py
+++ b/solution.py
@@ -11,7 +11,7 @@
 SNAPS = 128
 SHIFTS = 48
 BLOCK = 128
-GROUP = 2
+GROUP = 16
 ROW = ("row_0", "row_1")
 SHIFT = ("z", "core")
 EVERY = (*ROW, *SHIFT)
@@ -31,6 +31,10 @@
     )
 
 
+def near(x):
+    return pltpu.with_memory_space_constraint(x, pltpu.VMEM)
+
+
 def sent_to_all(x, axis):
     copies = jnp.broadcast_to(x, (lax.axis_size(axis), *x.shape))
     return lax.all_to_all(copies, axis, split_axis=0, concat_axis=0, tiled=True)
@@ -38,7 +42,7 @@
 
 def covariance_kernel(
     place, offsets, own, after, mirror, mirror_after, tail, pieces, basis,
-    cov, mapped, row_w, row_z, col_w, col_z, acc,
+    cov, cov_near, mapped, row_w, row_z, col_w, col_z, acc,
 ):
     r = place[0]
     c = place[1]
@@ -95,9 +99,10 @@
         acc[...] += dot_nt(jnp.concatenate(left, axis=1), jnp.concatenate(right, axis=1))
         return carry
 
-    lax.fori_loop(0, 16 // GROUP, step, 0)
+    step(0, 0)
     block = acc[...] * (1.0 / (SNAPS * SHIFTS))
     cov[...] = block
+    cov_near[...] = block
     image = dot_nn(basis[...], block, HIGH)
     for p in range(32):
         mapped[p] = image[4 * (p // 2) : 4 * (p // 2) + 4, SNAPS * (p % 2) : SNAPS * (p % 2) + SNAPS]
@@ -109,10 +114,11 @@
         covariance_kernel,
         name="covariance_block",
         in_specs=[pl.BlockSpec(memory_space=pltpu.SMEM)] * 2 + [vmem] * 7,
-        out_specs=[vmem, vmem],
+        out_specs=[vmem] * 3,
         out_shape=[
             jax.ShapeDtypeStruct((BLOCK, 2 * BLOCK), jnp.float32),
-            jax.ShapeDtypeStruct((32, 4, SNAPS), jnp.float32),
+            pltpu.VMEM((BLOCK, 2 * BLOCK), jnp.float32),
+            pltpu.VMEM((32, 4, SNAPS), jnp.float32),
         ],
         scratch_shapes=[
             pltpu.VMEM((2, 2 * BLOCK, SNAPS), jnp.float32),
@@ -121,7 +127,7 @@
             pltpu.VMEM((2, 3 * BLOCK, SNAPS), jnp.float32),
             pltpu.VMEM((BLOCK, 2 * BLOCK), jnp.float32),
         ],
-    )(place, offsets, own, after, mirror, mirror_after, tail, pieces, basis)
+    )(place, offsets, *[near(x) for x in (own, after, mirror, mirror_after, tail, pieces, basis)])
 
 
 def inverse_factor(gram):
@@ -196,13 +202,13 @@
     basis[...] = dot_nn(inverse_factor(halves_stacked(total)), mapped[...], HIGH)
 
 
-def local_call(kernel, shapes, *operands):
+def local_call(kernel, shapes, *operands, result=pltpu.VMEM):
     spaces = [pltpu.SMEM if x.dtype == jnp.int32 else pltpu.VMEM for x in operands]
     return pl.pallas_call(
         kernel,
         in_specs=[pl.BlockSpec(memory_space=space) for space in spaces],
-        out_shape=[jax.ShapeDtypeStruct(s, jnp.float32) for s in shapes],
-    )(*operands)
+        out_shape=[result(s, jnp.float32) for s in shapes],
+    )(*[x if x.dtype == jnp.int32 else near(x) for x in operands])
 
 
 def exchanged(tiles, axis):
@@ -241,16 +247,15 @@
     after = lax.ppermute(own, ROW, [(i, (i - 1) % 32) for i in range(32)])
     mirror = lax.ppermute(own, ROW, [(i, 31 - i) for i in range(32)])
     mirror_after = lax.ppermute(own, ROW, [(i, (32 - i) % 32) for i in range(32)])
-    pieces = sent_to_all(piece, "row_1")
-    pieces = sent_to_all(pieces, "row_0").reshape(32, 32, 2 * SNAPS)
+    pieces = sent_to_all(piece, ROW)
     every_offset = pieces[:16, 16, :3].astype(jnp.int32)
     place = jnp.stack([r, c]).astype(jnp.int32)
-    cov, mapped = covariance_block(
+    cov, cov_near, mapped = covariance_block(
         place, every_offset, own, after, mirror, mirror_after, tail, pieces, start_basis
     )
     mapped = total_over(mapped, ROW)
     half = (3 * K // 4, BLOCK)
-    kept, sent = local_call(image_kernel, [half, half], place, mapped, cov)
+    kept, sent = local_call(image_kernel, [half, half], place, mapped, cov_near)
     swap = [(0, 1), (1, 0)]
     mine = sent_to_all(kept + lax.ppermute(sent, "core", swap), "z").sum(axis=0)
     other = lax.ppermute(mine, "core", swap)
@@ -258,7 +263,7 @@
         first_factor_kernel, [(K, BLOCK), (4, K // 2, 2 * K)], place, mine, other
     )
     grams = sent_to_all(exchanged(grams, "row_0").sum(axis=0), "row_1")
-    (basis,) = local_call(last_factor_kernel, [(K, BLOCK)], grams, mapped)
+    (basis,) = local_call(last_factor_kernel, [(K, BLOCK)], grams, mapped, result=jax.ShapeDtypeStruct)
     return (cov, basis)
 
 

time: 153 us -> 137 us (0.90)
  blocking collectives: 84 us -> 67.3 us
  starting transfers between devices: 39.8 us -> 45 us
  Pallas kernels: 15.4 us -> 11.3 us
    all_to_all x4 -> x3, blocking collectives: 56.8 us -> 42.3 us  [sent_to_all(): return lax.all_to_all(copies, axis, split_axis=0, concat_axis=0, tiled=True)]
    all_to_all x1, starting transfers between devices: 3.6 us -> 7.28 us  [sent_to_all(): return lax.all_to_all(copies, axis, split_axis=0, concat_axis=0, tiled=True)]
    pallas_call x3, Pallas kernels: 8.77 us -> 6.16 us  [local_call(): pl.pallas_call(kernel, in_specs=[pl.BlockSpec(memory_space=space) for spa...]
    ppermute x1, starting transfers between devices: 4.13 us -> 6.55 us  [per_device(): after = lax.ppermute(own, ROW, [(i, (i - 1) % 32) for i in range(32)])]
    all_to_all x2, blocking collectives: 27.2 us -> 25 us  [exchanged(): return lax.all_to_all(tiles, axis, split_axis=0, concat_axis=0, tiled=True)]
    ppermute x1, starting transfers between devices: 10.2 us -> 8.55 us  [per_device(): mine = sent_to_all(kept + lax.ppermute(sent, 'core', swap), 'z').sum(axis=0)]
    all_to_all x1, waiting for transfers between devices: 0.01 us -> 1.55 us  [sent_to_all(): return lax.all_to_all(copies, axis, split_axis=0, concat_axis=0, tiled=True)]
  transfers between devices with their start and end apart: 7 -> 7, of which waited for: 4 -> 5; matrix products, arithmetic and copies ran while one was open for 1% -> 1% of each run, Pallas kernels for 0% -> 0%
where the time goes in v1:
time: 137 us; the launch traced here: 136 us
  blocking collectives  67.3 us (49%)
  starting transfers between devices  45 us (33%)
  Pallas kernels  11.3 us (8%)
  waiting for transfers between devices  7.78 us (6%)
  local copies, waits for them, and re-layouts  2.36 us (2%)
    all_to_all x3, blocking collectives, sent_to_all(): return lax.all_to_all(copies, axis, split_axis=0, concat_axis=0, tiled=True)  42.3 us
    all_to_all x2, blocking collectives, exchanged(): return lax.all_to_all(tiles, axis, split_axis=0, concat_axis=0, tiled=True)  25 us
    ppermute x1, starting transfers between devices, per_device(): piece = lax.ppermute(piece, EVERY, piece_routes())  15 us
    ppermute x1, starting transfers between devices, per_device(): mine = sent_to_all(kept + lax.ppermute(sent, 'core', swap), 'z').sum(axis=0)  8.55 us
    all_to_all x1, starting transfers between devices, sent_to_all(): return lax.all_to_all(copies, axis, split_axis=0, concat_axis=0, tiled=True)  7.28 us
    ppermute x1, starting transfers between devices, per_device(): after = lax.ppermute(own, ROW, [(i, (i - 1) % 32) for i in range(32)])  6.55 us
    pallas_call x3, Pallas kernels, local_call(): pl.pallas_call(kernel, in_specs=[pl.BlockSpec(memory_space=space) for spa...  6.16 us
    pallas_call x1, Pallas kernels, covariance_block(): pl.pallas_call(covariance_kernel, name='covariance_block', in_specs=[pl.B...  5.09 us
  transfers between devices with their start and end apart: 7, of which 5 were waited for; matrix products, arithmetic and copies ran while one was open for 1% of the time, Pallas kernels for 0%

profile of v1, /device:TPU:1, one launch (start us, length us, event | category | flops | bytes accessed | tf_op | source)
XLA Modules:
  0.0 135.7 jit_solution(2608542610235479247)
XLA Ops:
  0.6 0.0 copy-start.1
  0.7 0.8 copy-done.1
  1.5 0.0 copy-start.3
  1.5 0.6 copy-done.3
  2.1 15.0 %collective-permute-start = (bf16[32,256]{1,0:T(8,128)(2,1)S(1)}, bf16[32,256]{1,0:T(8,128)(2,1)S(1)}, u32[]{:S(2)}, u32[]{:S(2)}) collective-permute-start(bf16[32,256]{1,0:T(8,128)(2,1)S(1)} %fusion.2), channel_id=1, source_target_pairs={{0,256},{1,287},{2,303},{3,304},{4,320},{5,351},{6,367},{7,368},{8... | collective-permute-start | bytes 49160 | tf_op jit(solution)/shard_map/ppermute | solution.py:246
  17.1 0.8 collective-permute-done
  18.0 0.9 broadcast_in_dim.17
  18.8 0.0 copy-start.2
  18.8 7.3 %all-to-all-start = ((bf16[32,32,256]{2,1,0:T(8,128)(2,1)}), bf16[32,32,256]{2,1,0:T(8,128)(2,1)S(1)}, u32[]{:S(2)}, u32[]{:S(2)}) async-start(bf16[32,32,256]{2,1,0:T(8,128)(2,1)} %broadcast_in_dim.17), calls=%async_computation | async-start | bytes 1048576 | tf_op jit(solution)/shard_map/all_to_all | solution.py:40
  26.1 6.6 %collective-permute-start.1 = (bf16[128,256]{1,0:T(8,128)(2,1)S(1)}, bf16[128,256]{1,0:T(8,128)(2,1)S(1)}, u32[]{:S(2)}, u32[]{:S(2)}) collective-permute-start(bf16[128,256]{1,0:T(8,128)(2,1)S(1)} %bitcast.15), channel_id=1, source_target_pairs={{0,496},{16,0},{32,16},{48,32},{64,48},{80,64},{96,80},{112,96},{1... | collective-permute-start | bytes 196616 | tf_op jit(solution)/shard_map/ppermute | solution.py:247
  32.7 3.1 %collective-permute-start.2 = (bf16[128,256]{1,0:T(8,128)(2,1)S(1)}, bf16[128,256]{1,0:T(8,128)(2,1)S(1)}, u32[]{:S(2)}, u32[]{:S(2)}) collective-permute-start(bf16[128,256]{1,0:T(8,128)(2,1)S(1)} %bitcast.16), channel_id=1, source_target_pairs={{0,496},{16,480},{32,464},{48,448},{64,432},{80,416},{96,400},{112... | collective-permute-start | bytes 196616 | tf_op jit(solution)/shard_map/ppermute | solution.py:248
  35.8 0.7 collective-permute-start.3
  36.4 0.0 copy-done.2
  36.4 0.0 copy-start
  36.5 0.6 pad_add_fusion.place
  37.0 1.6 %all-to-all-done.pieces = bf16[32,32,256]{2,1,0:T(8,128)(2,1)S(1)} async-done(((bf16[32,32,256]{2,1,0:T(8,128)(2,1)}), bf16[32,32,256]{2,1,0:T(8,128)(2,1)S(1)}, u32[]{:S(2)}, u32[]{:S(2)}) %all-to-all-start) | async-done | bytes 524320 | tf_op jit(solution)/shard_map/all_to_all | solution.py:40
  38.6 0.6 slice_convert_fusion
  39.2 0.0 collective-permute-done.1.after
  39.2 3.7 %collective-permute-done.2.mirror = bf16[128,256]{1,0:T(8,128)(2,1)S(1)} collective-permute-done((bf16[128,256]{1,0:T(8,128)(2,1)S(1)}, bf16[128,256]{1,0:T(8,128)(2,1)S(1)}, u32[]{:S(2)}, u32[]{:S(2)}) %collective-permute-start.2) | collective-permute-done | bytes 65568 | tf_op jit(solution)/shard_map/ppermute | solution.py:248
  42.9 0.0 collective-permute-done.3.mirror_after
  42.9 0.0 copy-done
  42.9 5.1 %covariance_block.1 = (f32[128,256]{1,0:T(8,128)}, f32[128,256]{1,0:T(8,128)S(1)}, f32[32,4,128]{2,1,0:T(4,128)S(1)}) custom-call(s32[2]{0:T(128)} %pad_add_fusion.place, s32[16,3]{1,0:T(8,128)} %bitcast.22, bf16[128,256]{1,0:T(8,128)(2,1)S(1)} %bitcast.18, bf16[128,256]{1,0:T(8,128)(2,1)S(1)} %collective-permute-done.1.after, ...), custom_call_target="tpu_custom_call" | custom-call | tf_op jit(solution)/shard_map/covariance_block/pallas_call | solution.py:113
  48.0 18.1 %all_to_all.30 = f32[32,4,128]{2,1,0:T(4,128)S(1)} all-to-all(f32[32,4,128]{2,1,0:T(4,128)S(1)} %get-tuple-element.10), channel_id=1, replica_groups=mesh['row_0'=4,'row_1'=8,'z'=8,'core'=2] {'row_0','row_1'}, dimensions={0} | all-to-all | bytes 131072 | tf_op jit(solution)/shard_map/all_to_all | solution.py:215
  66.2 11.8 %all_to_all.31.mapped = f32[32,4,128]{2,1,0:T(4,128)S(1)} all-to-all(f32[32,4,128]{2,1,0:T(4,128)S(1)} %broadcast_in_dim.18), channel_id=1, replica_groups=mesh['row_0'=4,'row_1'=8,'z'=8,'core'=2] {'row_0','row_1'}, dimensions={0} | all-to-all | bytes 131072 | tf_op jit(solution)/shard_map/all_to_all | solution.py:40
  78.0 1.0 shard_map.59
  79.0 8.6 %collective-permute-start.4 = (f32[48,128]{1,0:T(8,128)S(1)}, f32[48,128]{1,0:T(8,128)S(1)}, u32[]{:S(2)}, u32[]{:S(2)}) collective-permute-start(f32[48,128]{1,0:T(8,128)S(1)} %get-tuple-element.13), channel_id=1, source_target_pairs={{0,1},{1,0},{2,3},{3,2},{4,5},{5,4},{6,7},{7,6},{8,9},{9,8},{10,11... | collective-permute-start | bytes 73736 | tf_op jit(solution)/shard_map/ppermute | solution.py:260
  87.6 0.8 collective-permute-done.4
  88.4 20.1 %all_to_all.32 = f32[8,48,128]{2,1,0:T(8,128)S(1)} all-to-all(f32[8,48,128]{2,1,0:T(8,128)S(1)} %broadcast_in_dim.19), channel_id=1, replica_groups=mesh['row_0'=4,'row_1'=8,'z'=8,'core'=2] {'z'}, dimensions={0} | all-to-all | bytes 393216 | tf_op jit(solution)/shard_map/all_to_all | solution.py:40
  108.6 3.9 %collective-permute-start.5 = (f32[48,128]{1,0:T(8,128)S(1)}, f32[48,128]{1,0:T(8,128)S(1)}, u32[]{:S(2)}, u32[]{:S(2)}) collective-permute-start(f32[48,128]{1,0:T(8,128)S(1)} %reduce_sum.28.mine), channel_id=1, source_target_pairs={{0,1},{1,0},{2,3},{3,2},{4,5},{5,4},{6,7},{7,6},{8,9},{9,8},{10,11... | collective-permute-start | bytes 73736 | tf_op jit(solution)/shard_map/ppermute | solution.py:261
  112.5 0.8 collective-permute-done.5.other
  113.3 2.7 %shard_map.60 = (f32[64,128]{1,0:T(8,128)S(1)}, f32[4,32,128]{2,1,0:T(8,128)S(1)}) custom-call(s32[2]{0:T(128)} %pad_add_fusion.place, f32[48,128]{1,0:T(8,128)S(1)} %reduce_sum.28.mine, f32[48,128]{1,0:T(8,128)S(1)} %collective-permute-done.5.other), custom_call_target="tpu_custom_call" | custom-call | tf_op jit(solution)/shard_map/pallas_call | solution.py:207
  116.0 6.9 %all_to_all.33 = f32[4,32,128]{2,1,0:T(8,128)S(1)} all-to-all(f32[4,32,128]{2,1,0:T(8,128)S(1)} %get-tuple-element.14), channel_id=1, replica_groups=mesh['row_0'=4,'row_1'=8,'z'=8,'core'=2] {'row_0'}, dimensions={0} | all-to-all | bytes 131072 | tf_op jit(solution)/shard_map/all_to_all | solution.py:215
  122.9 10.3 %all_to_all.34.grams = f32[8,32,128]{2,1,0:T(8,128)S(1)} all-to-all(f32[8,32,128]{2,1,0:T(8,128)S(1)} %broadcast_in_dim.20), channel_id=1, replica_groups=mesh['row_0'=4,'row_1'=8,'z'=8,'core'=2] {'row_1'}, dimensions={0} | all-to-all | bytes 262144 | tf_op jit(solution)/shard_map/all_to_all | solution.py:40
  133.3 2.4 %shard_map.61 = f32[64,128]{1,0:T(8,128)} custom-call(f32[8,32,128]{2,1,0:T(8,128)S(1)} %all_to_all.34.grams, f32[64,128]{1,0:T(8,128)S(1)} %get-tuple-element.15.mapped), custom_call_target="tpu_custom_call" | custom-call | tf_op jit(solution)/shard_map/pallas_call | solution.py:207
  (12 shorter events, 0.2 us)
Async XLA Ops:
  0.6 0.8 copy-start.1
  1.5 0.7 copy-start.3
  2.1 15.8 %collective-permute-start = (bf16[32,256]{1,0:T(8,128)(2,1)S(1)}, bf16[32,256]{1,0:T(8,128)(2,1)S(1)}, u32[]{:S(2)}, u32[]{:S(2)}) collective-permute-start(bf16[32,256]{1,0:T(8,128)(2,1)S(1)} %fusion.2), channel_id=1, source_target_pairs={{0,256},{1,287},{2,303},{3,304},{4,320},{5,351},{6,367},{7,368},{8... | collective-permute-start | bytes 49160 | tf_op jit(solution)/shard_map/ppermute | solution.py:246
  18.8 17.6 %copy-start.2 = (bf16[128,2,128]{2,1,0:T(2,128)(2,1)S(1)}, bf16[128,2,128]{2,1,0:T(2,128)(2,1)}, u32[]{:S(2)}) copy-start(bf16[128,2,128]{2,1,0:T(2,128)(2,1)} %param.5) | copy-start | bytes 196612
  18.8 19.8 %all-to-all-start = ((bf16[32,32,256]{2,1,0:T(8,128)(2,1)}), bf16[32,32,256]{2,1,0:T(8,128)(2,1)S(1)}, u32[]{:S(2)}, u32[]{:S(2)}) async-start(bf16[32,32,256]{2,1,0:T(8,128)(2,1)} %broadcast_in_dim.17), calls=%async_computation | async-start | bytes 1048576 | tf_op jit(solution)/shard_map/all_to_all | solution.py:40
  26.1 13.1 %collective-permute-start.1 = (bf16[128,256]{1,0:T(8,128)(2,1)S(1)}, bf16[128,256]{1,0:T(8,128)(2,1)S(1)}, u32[]{:S(2)}, u32[]{:S(2)}) collective-permute-start(bf16[128,256]{1,0:T(8,128)(2,1)S(1)} %bitcast.15), channel_id=1, source_target_pairs={{0,496},{16,0},{32,16},{48,32},{64,48},{80,64},{96,80},{112,96},{1... | collective-permute-start | bytes 196616 | tf_op jit(solution)/shard_map/ppermute | solution.py:247
  32.7 10.3 %collective-permute-start.2 = (bf16[128,256]{1,0:T(8,128)(2,1)S(1)}, bf16[128,256]{1,0:T(8,128)(2,1)S(1)}, u32[]{:S(2)}, u32[]{:S(2)}) collective-permute-start(bf16[128,256]{1,0:T(8,128)(2,1)S(1)} %bitcast.16), channel_id=1, source_target_pairs={{0,496},{16,480},{32,464},{48,448},{64,432},{80,416},{96,400},{112... | collective-permute-start | bytes 196616 | tf_op jit(solution)/shard_map/ppermute | solution.py:248
  35.8 7.2 %collective-permute-start.3 = (bf16[128,256]{1,0:T(8,128)(2,1)S(1)}, bf16[128,256]{1,0:T(8,128)(2,1)S(1)}, u32[]{:S(2)}, u32[]{:S(2)}) collective-permute-start(bf16[128,256]{1,0:T(8,128)(2,1)S(1)} %bitcast.17), channel_id=1, source_target_pairs={{0,0},{16,496},{32,480},{48,464},{64,448},{80,432},{96,416},{112,4... | collective-permute-start | bytes 196616 | tf_op jit(solution)/shard_map/ppermute | solution.py:249
  36.4 6.5 %copy-start = (f32[64,128]{1,0:T(8,128)S(1)}, f32[64,128]{1,0:T(8,128)}, u32[]{:S(2)}) copy-start(f32[64,128]{1,0:T(8,128)} %basis.1) | copy-start | bytes 98308
  79.0 9.4 %collective-permute-start.4 = (f32[48,128]{1,0:T(8,128)S(1)}, f32[48,128]{1,0:T(8,128)S(1)}, u32[]{:S(2)}, u32[]{:S(2)}) collective-permute-start(f32[48,128]{1,0:T(8,128)S(1)} %get-tuple-element.13), channel_id=1, source_target_pairs={{0,1},{1,0},{2,3},{3,2},{4,5},{5,4},{6,7},{7,6},{8,9},{9,8},{10,11... | collective-permute-start | bytes 73736 | tf_op jit(solution)/shard_map/ppermute | solution.py:260
  108.6 4.7 %collective-permute-start.5 = (f32[48,128]{1,0:T(8,128)S(1)}, f32[48,128]{1,0:T(8,128)S(1)}, u32[]{:S(2)}, u32[]{:S(2)}) collective-permute-start(f32[48,128]{1,0:T(8,128)S(1)} %reduce_sum.28.mine), channel_id=1, source_target_pairs={{0,1},{1,0},{2,3},{3,2},{4,5},{5,4},{6,7},{7,6},{8,9},{9,8},{10,11... | collective-permute-start | bytes 73736 | tf_op jit(solution)/shard_map/ppermute | solution.py:261

commit v2 on v1

--- a/solution.py
+++ b/solution.py
@@ -38,6 +38,17 @@
 def sent_to_all(x, axis):
     copies = jnp.broadcast_to(x, (lax.axis_size(axis), *x.shape))
     return lax.all_to_all(copies, axis, split_axis=0, concat_axis=0, tiled=True)
+
+
+def copies_kernel(piece, copies):
+    for i in range(copies.shape[0]):
+        copies[i] = piece[...]
+
+
+def copies_of(piece, count):
+    return pl.pallas_call(
+        copies_kernel, name="copies", out_shape=pltpu.VMEM((count, *piece.shape), piece.dtype)
+    )(near(piece))
 
 
 def covariance_kernel(
@@ -247,7 +258,7 @@
     after = lax.ppermute(own, ROW, [(i, (i - 1) % 32) for i in range(32)])
     mirror = lax.ppermute(own, ROW, [(i, 31 - i) for i in range(32)])
     mirror_after = lax.ppermute(own, ROW, [(i, (32 - i) % 32) for i in range(32)])
-    pieces = sent_to_all(piece, ROW)
+    pieces = exchanged(copies_of(piece, lax.axis_size(ROW)), ROW)
     every_offset = pieces[:16, 16, :3].astype(jnp.int32)
     place = jnp.stack([r, c]).astype(jnp.int32)
     cov, cov_near, mapped = covariance_block(

time: 137 us -> 137 us (level)
  no operation moved by 1% of the time
where the time goes in v2:
time: 137 us; the launch traced here: 136 us
  blocking collectives  67.3 us (49%)
  starting transfers between devices  45 us (33%)
  Pallas kernels  12.1 us (9%)
  waiting for transfers between devices  7.78 us (6%)
  local copies, waits for them, and re-layouts  1.5 us (1%)
    all_to_all x3, blocking collectives, sent_to_all(): return lax.all_to_all(copies, axis, split_axis=0, concat_axis=0, tiled=True)  42.3 us
    all_to_all x2, blocking collectives, exchanged(): return lax.all_to_all(tiles, axis, split_axis=0, concat_axis=0, tiled=True)  25 us
    ppermute x1, starting transfers between devices, per_device(): piece = lax.ppermute(piece, EVERY, piece_routes())  15 us
    ppermute x1, starting transfers between devices, per_device(): mine = sent_to_all(kept + lax.ppermute(sent, 'core', swap), 'z').sum(axis=0)  8.55 us
    all_to_all x1, starting transfers between devices, exchanged(): return lax.all_to_all(tiles, axis, split_axis=0, concat_axis=0, tiled=True)  7.28 us
    ppermute x1, starting transfers between devices, per_device(): after = lax.ppermute(own, ROW, [(i, (i - 1) % 32) for i in range(32)])  6.55 us
    pallas_call x3, Pallas kernels, local_call(): pl.pallas_call(kernel, in_specs=[pl.BlockSpec(memory_space=space) for spa...  6.16 us
    pallas_call x1, Pallas kernels, covariance_block(): pl.pallas_call(covariance_kernel, name='covariance_block', in_specs=[pl.B...  5.09 us
  transfers between devices with their start and end apart: 7, of which 5 were waited for; matrix products, arithmetic and copies ran while one was open for 1% of the time, Pallas kernels for 0%

profile of v2, /device:TPU:1, one launch (start us, length us, event | category | flops | bytes accessed | tf_op | source)
XLA Modules:
  0.0 135.7 jit_solution(11659879474924566272)
XLA Ops:
  0.6 0.0 copy-start.1
  0.7 0.8 copy-done.1
  1.5 0.0 copy-start.3
  1.5 0.6 copy-done.3
  2.1 15.0 %collective-permute-start = (bf16[32,256]{1,0:T(8,128)(2,1)S(1)}, bf16[32,256]{1,0:T(8,128)(2,1)S(1)}, u32[]{:S(2)}, u32[]{:S(2)}) collective-permute-start(bf16[32,256]{1,0:T(8,128)(2,1)S(1)} %fusion.2), channel_id=1, source_target_pairs={{0,256},{1,287},{2,303},{3,304},{4,320},{5,351},{6,367},{7,368},{8... | collective-permute-start | bytes 49160 | tf_op jit(solution)/shard_map/ppermute | solution.py:257
  17.1 0.8 collective-permute-done.piece
  18.0 0.8 copies.1
  18.8 0.0 copy-start.2
  18.8 7.3 %all-to-all-start = ((bf16[32,32,256]{2,1,0:T(8,128)(2,1)}), bf16[32,32,256]{2,1,0:T(8,128)(2,1)S(1)}, u32[]{:S(2)}, u32[]{:S(2)}) async-start(bf16[32,32,256]{2,1,0:T(8,128)(2,1)} %copies.1), calls=%async_computation | async-start | bytes 1048576 | tf_op jit(solution)/shard_map/all_to_all | solution.py:226
  26.1 6.6 %collective-permute-start.1 = (bf16[128,256]{1,0:T(8,128)(2,1)S(1)}, bf16[128,256]{1,0:T(8,128)(2,1)S(1)}, u32[]{:S(2)}, u32[]{:S(2)}) collective-permute-start(bf16[128,256]{1,0:T(8,128)(2,1)S(1)} %bitcast.15), channel_id=1, source_target_pairs={{0,496},{16,0},{32,16},{48,32},{64,48},{80,64},{96,80},{112,96},{1... | collective-permute-start | bytes 196616 | tf_op jit(solution)/shard_map/ppermute | solution.py:258
  32.6 3.1 %collective-permute-start.2 = (bf16[128,256]{1,0:T(8,128)(2,1)S(1)}, bf16[128,256]{1,0:T(8,128)(2,1)S(1)}, u32[]{:S(2)}, u32[]{:S(2)}) collective-permute-start(bf16[128,256]{1,0:T(8,128)(2,1)S(1)} %bitcast.16), channel_id=1, source_target_pairs={{0,496},{16,480},{32,464},{48,448},{64,432},{80,416},{96,400},{112... | collective-permute-start | bytes 196616 | tf_op jit(solution)/shard_map/ppermute | solution.py:259
  35.7 0.7 collective-permute-start.3
  36.4 0.0 copy-done.2
  36.4 0.0 copy-start
  36.4 0.6 pad_add_fusion.place
  37.0 1.6 %all-to-all-done.pieces = bf16[32,32,256]{2,1,0:T(8,128)(2,1)S(1)} async-done(((bf16[32,32,256]{2,1,0:T(8,128)(2,1)}), bf16[32,32,256]{2,1,0:T(8,128)(2,1)S(1)}, u32[]{:S(2)}, u32[]{:S(2)}) %all-to-all-start) | async-done | bytes 524320 | tf_op jit(solution)/shard_map/all_to_all | solution.py:226
  38.6 0.6 slice_convert_fusion
  39.2 0.0 collective-permute-done.1.after
  39.2 3.7 %collective-permute-done.2.mirror = bf16[128,256]{1,0:T(8,128)(2,1)S(1)} collective-permute-done((bf16[128,256]{1,0:T(8,128)(2,1)S(1)}, bf16[128,256]{1,0:T(8,128)(2,1)S(1)}, u32[]{:S(2)}, u32[]{:S(2)}) %collective-permute-start.2) | collective-permute-done | bytes 65568 | tf_op jit(solution)/shard_map/ppermute | solution.py:259
  42.9 0.0 collective-permute-done.3.mirror_after
  42.9 0.0 copy-done
  42.9 5.1 %covariance_block.1 = (f32[128,256]{1,0:T(8,128)}, f32[128,256]{1,0:T(8,128)S(1)}, f32[32,4,128]{2,1,0:T(4,128)S(1)}) custom-call(s32[2]{0:T(128)} %pad_add_fusion.place, s32[16,3]{1,0:T(8,128)} %bitcast.22, bf16[128,256]{1,0:T(8,128)(2,1)S(1)} %bitcast.18, bf16[128,256]{1,0:T(8,128)(2,1)S(1)} %collective-permute-done.1.after, ...), custom_call_target="tpu_custom_call" | custom-call | tf_op jit(solution)/shard_map/covariance_block/pallas_call | solution.py:124
  48.0 18.1 %all_to_all.30 = f32[32,4,128]{2,1,0:T(4,128)S(1)} all-to-all(f32[32,4,128]{2,1,0:T(4,128)S(1)} %get-tuple-element.10), channel_id=1, replica_groups=mesh['row_0'=4,'row_1'=8,'z'=8,'core'=2] {'row_0','row_1'}, dimensions={0} | all-to-all | bytes 131072 | tf_op jit(solution)/shard_map/all_to_all | solution.py:226
  66.2 11.8 %all_to_all.31.mapped = f32[32,4,128]{2,1,0:T(4,128)S(1)} all-to-all(f32[32,4,128]{2,1,0:T(4,128)S(1)} %broadcast_in_dim.14), channel_id=1, replica_groups=mesh['row_0'=4,'row_1'=8,'z'=8,'core'=2] {'row_0','row_1'}, dimensions={0} | all-to-all | bytes 131072 | tf_op jit(solution)/shard_map/all_to_all | solution.py:40
  78.0 1.0 shard_map.59
  79.0 8.6 %collective-permute-start.4 = (f32[48,128]{1,0:T(8,128)S(1)}, f32[48,128]{1,0:T(8,128)S(1)}, u32[]{:S(2)}, u32[]{:S(2)}) collective-permute-start(f32[48,128]{1,0:T(8,128)S(1)} %get-tuple-element.13), channel_id=1, source_target_pairs={{0,1},{1,0},{2,3},{3,2},{4,5},{5,4},{6,7},{7,6},{8,9},{9,8},{10,11... | collective-permute-start | bytes 73736 | tf_op jit(solution)/shard_map/ppermute | solution.py:271
  87.6 0.8 collective-permute-done.4
  88.4 20.1 %all_to_all.32 = f32[8,48,128]{2,1,0:T(8,128)S(1)} all-to-all(f32[8,48,128]{2,1,0:T(8,128)S(1)} %broadcast_in_dim.15), channel_id=1, replica_groups=mesh['row_0'=4,'row_1'=8,'z'=8,'core'=2] {'z'}, dimensions={0} | all-to-all | bytes 393216 | tf_op jit(solution)/shard_map/all_to_all | solution.py:40
  108.6 3.9 %collective-permute-start.5 = (f32[48,128]{1,0:T(8,128)S(1)}, f32[48,128]{1,0:T(8,128)S(1)}, u32[]{:S(2)}, u32[]{:S(2)}) collective-permute-start(f32[48,128]{1,0:T(8,128)S(1)} %reduce_sum.28.mine), channel_id=1, source_target_pairs={{0,1},{1,0},{2,3},{3,2},{4,5},{5,4},{6,7},{7,6},{8,9},{9,8},{10,11... | collective-permute-start | bytes 73736 | tf_op jit(solution)/shard_map/ppermute | solution.py:272
  112.4 0.8 collective-permute-done.5.other
  113.3 2.7 %shard_map.60 = (f32[64,128]{1,0:T(8,128)S(1)}, f32[4,32,128]{2,1,0:T(8,128)S(1)}) custom-call(s32[2]{0:T(128)} %pad_add_fusion.place, f32[48,128]{1,0:T(8,128)S(1)} %reduce_sum.28.mine, f32[48,128]{1,0:T(8,128)S(1)} %collective-permute-done.5.other), custom_call_target="tpu_custom_call" | custom-call | tf_op jit(solution)/shard_map/pallas_call | solution.py:218
  116.0 6.9 %all_to_all.33 = f32[4,32,128]{2,1,0:T(8,128)S(1)} all-to-all(f32[4,32,128]{2,1,0:T(8,128)S(1)} %get-tuple-element.14), channel_id=1, replica_groups=mesh['row_0'=4,'row_1'=8,'z'=8,'core'=2] {'row_0'}, dimensions={0} | all-to-all | bytes 131072 | tf_op jit(solution)/shard_map/all_to_all | solution.py:226
  122.9 10.3 %all_to_all.34.grams = f32[8,32,128]{2,1,0:T(8,128)S(1)} all-to-all(f32[8,32,128]{2,1,0:T(8,128)S(1)} %broadcast_in_dim.16), channel_id=1, replica_groups=mesh['row_0'=4,'row_1'=8,'z'=8,'core'=2] {'row_1'}, dimensions={0} | all-to-all | bytes 262144 | tf_op jit(solution)/shard_map/all_to_all | solution.py:40
  133.2 2.4 %shard_map.61 = f32[64,128]{1,0:T(8,128)} custom-call(f32[8,32,128]{2,1,0:T(8,128)S(1)} %all_to_all.34.grams, f32[64,128]{1,0:T(8,128)S(1)} %get-tuple-element.15.mapped), custom_call_target="tpu_custom_call" | custom-call | tf_op jit(solution)/shard_map/pallas_call | solution.py:218
  (12 shorter events, 0.2 us)
Async XLA Ops:
  0.6 0.8 copy-start.1
  1.5 0.7 copy-start.3
  2.1 15.8 %collective-permute-start = (bf16[32,256]{1,0:T(8,128)(2,1)S(1)}, bf16[32,256]{1,0:T(8,128)(2,1)S(1)}, u32[]{:S(2)}, u32[]{:S(2)}) collective-permute-start(bf16[32,256]{1,0:T(8,128)(2,1)S(1)} %fusion.2), channel_id=1, source_target_pairs={{0,256},{1,287},{2,303},{3,304},{4,320},{5,351},{6,367},{7,368},{8... | collective-permute-start | bytes 49160 | tf_op jit(solution)/shard_map/ppermute | solution.py:257
  18.8 17.6 %copy-start.2 = (bf16[128,2,128]{2,1,0:T(2,128)(2,1)S(1)}, bf16[128,2,128]{2,1,0:T(2,128)(2,1)}, u32[]{:S(2)}) copy-start(bf16[128,2,128]{2,1,0:T(2,128)(2,1)} %param.5) | copy-start | bytes 196612
  18.8 19.8 %all-to-all-start = ((bf16[32,32,256]{2,1,0:T(8,128)(2,1)}), bf16[32,32,256]{2,1,0:T(8,128)(2,1)S(1)}, u32[]{:S(2)}, u32[]{:S(2)}) async-start(bf16[32,32,256]{2,1,0:T(8,128)(2,1)} %copies.1), calls=%async_computation | async-start | bytes 1048576 | tf_op jit(solution)/shard_map/all_to_all | solution.py:226
  26.1 13.1 %collective-permute-start.1 = (bf16[128,256]{1,0:T(8,128)(2,1)S(1)}, bf16[128,256]{1,0:T(8,128)(2,1)S(1)}, u32[]{:S(2)}, u32[]{:S(2)}) collective-permute-start(bf16[128,256]{1,0:T(8,128)(2,1)S(1)} %bitcast.15), channel_id=1, source_target_pairs={{0,496},{16,0},{32,16},{48,32},{64,48},{80,64},{96,80},{112,96},{1... | collective-permute-start | bytes 196616 | tf_op jit(solution)/shard_map/ppermute | solution.py:258
  32.6 10.3 %collective-permute-start.2 = (bf16[128,256]{1,0:T(8,128)(2,1)S(1)}, bf16[128,256]{1,0:T(8,128)(2,1)S(1)}, u32[]{:S(2)}, u32[]{:S(2)}) collective-permute-start(bf16[128,256]{1,0:T(8,128)(2,1)S(1)} %bitcast.16), channel_id=1, source_target_pairs={{0,496},{16,480},{32,464},{48,448},{64,432},{80,416},{96,400},{112... | collective-permute-start | bytes 196616 | tf_op jit(solution)/shard_map/ppermute | solution.py:259
  35.7 7.2 %collective-permute-start.3 = (bf16[128,256]{1,0:T(8,128)(2,1)S(1)}, bf16[128,256]{1,0:T(8,128)(2,1)S(1)}, u32[]{:S(2)}, u32[]{:S(2)}) collective-permute-start(bf16[128,256]{1,0:T(8,128)(2,1)S(1)} %bitcast.17), channel_id=1, source_target_pairs={{0,0},{16,496},{32,480},{48,464},{64,448},{80,432},{96,416},{112,4... | collective-permute-start | bytes 196616 | tf_op jit(solution)/shard_map/ppermute | solution.py:260
  36.4 6.5 %copy-start = (f32[64,128]{1,0:T(8,128)S(1)}, f32[64,128]{1,0:T(8,128)}, u32[]{:S(2)}) copy-start(f32[64,128]{1,0:T(8,128)} %basis.1) | copy-start | bytes 98308
  79.0 9.4 %collective-permute-start.4 = (f32[48,128]{1,0:T(8,128)S(1)}, f32[48,128]{1,0:T(8,128)S(1)}, u32[]{:S(2)}, u32[]{:S(2)}) collective-permute-start(f32[48,128]{1,0:T(8,128)S(1)} %get-tuple-element.13), channel_id=1, source_target_pairs={{0,1},{1,0},{2,3},{3,2},{4,5},{5,4},{6,7},{7,6},{8,9},{9,8},{10,11... | collective-permute-start | bytes 73736 | tf_op jit(solution)/shard_map/ppermute | solution.py:271
  108.6 4.7 %collective-permute-start.5 = (f32[48,128]{1,0:T(8,128)S(1)}, f32[48,128]{1,0:T(8,128)S(1)}, u32[]{:S(2)}, u32[]{:S(2)}) collective-permute-start(f32[48,128]{1,0:T(8,128)S(1)} %reduce_sum.28.mine), channel_id=1, source_target_pairs={{0,1},{1,0},{2,3},{3,2},{4,5},{5,4},{6,7},{7,6},{8,9},{9,8},{10,11... | collective-permute-start | bytes 73736 | tf_op jit(solution)/shard_map/ppermute | solution.py:272

commit v3 on v1

--- a/solution.py
+++ b/solution.py
@@ -17,6 +17,7 @@
 EVERY = (*ROW, *SHIFT)
 HALF_ROOT = 0.7071067811865476
 HIGH = lax.Precision.HIGHEST
+CORES_SWAPPED = [(0, 1), (1, 0)]
 
 
 def dot_nt(a, b, precision=None):
@@ -41,7 +42,7 @@
 
 
 def covariance_kernel(
-    place, offsets, own, after, mirror, mirror_after, tail, pieces, basis,
+    place, offsets, own, mine, other, tail, pieces, basis,
     cov, cov_near, mapped, row_w, row_z, col_w, col_z, acc,
 ):
     r = place[0]
@@ -65,11 +66,18 @@
         ref[0, pl.ds(at, BLOCK), :] = jnp.where(upper, re, -im)
         ref[1, pl.ds(at, BLOCK), :] = jnp.where(upper, im, re)
 
+    first = c % 2 == 0
+    after, mirror, mirror_after = (
+        jnp.concatenate(
+            [jnp.where(first, mine[i], other[i]), jnp.where(first, other[i], mine[i])], axis=0
+        )
+        for i in range(3)
+    )
     row_upper = r < 16
     put_window(row_w, 0, own[...], row_upper)
-    put_window(row_w, BLOCK, jnp.where(r == 31, tail[...], after[...]), row_upper)
-    put_mirror(row_z, 0, jnp.where(r == 0, tail[...], mirror_after[...]), row_upper)
-    put_mirror(row_z, BLOCK, mirror[...], row_upper)
+    put_window(row_w, BLOCK, jnp.where(r == 31, tail[...], after), row_upper)
+    put_mirror(row_z, 0, jnp.where(r == 0, tail[...], mirror_after), row_upper)
+    put_mirror(row_z, BLOCK, mirror, row_upper)
 
     odd = [jnp.concatenate([pieces[2 * i + j, :16, :] for i in range(8)], axis=0) for j in range(2)]
     even = [jnp.concatenate([pieces[16 + 4 * i + j] for i in range(4)], axis=0) for j in range(4)]
@@ -108,12 +116,12 @@
         mapped[p] = image[4 * (p // 2) : 4 * (p // 2) + 4, SNAPS * (p % 2) : SNAPS * (p % 2) + SNAPS]
 
 
-def covariance_block(place, offsets, own, after, mirror, mirror_after, tail, pieces, basis):
+def covariance_block(place, offsets, own, mine, other, tail, pieces, basis):
     vmem = pl.BlockSpec(memory_space=pltpu.VMEM)
     return pl.pallas_call(
         covariance_kernel,
         name="covariance_block",
-        in_specs=[pl.BlockSpec(memory_space=pltpu.SMEM)] * 2 + [vmem] * 7,
+        in_specs=[pl.BlockSpec(memory_space=pltpu.SMEM)] * 2 + [vmem] * 6,
         out_specs=[vmem] * 3,
         out_shape=[
             jax.ShapeDtypeStruct((BLOCK, 2 * BLOCK), jnp.float32),
@@ -127,7 +135,7 @@
             pltpu.VMEM((2, 3 * BLOCK, SNAPS), jnp.float32),
             pltpu.VMEM((BLOCK, 2 * BLOCK), jnp.float32),
         ],
-    )(place, offsets, *[near(x) for x in (own, after, mirror, mirror_after, tail, pieces, basis)])
+    )(place, offsets, *[near(x) for x in (own, mine, other, tail, pieces, basis)])
 
 
 def inverse_factor(gram):
@@ -244,21 +252,23 @@
     even_piece = lax.dynamic_slice_in_dim(own, 32 * (c // 4), 32, 0)
     piece = jnp.where(r % 2 == 1, odd_piece, even_piece)
     piece = lax.ppermute(piece, EVERY, piece_routes())
-    after = lax.ppermute(own, ROW, [(i, (i - 1) % 32) for i in range(32)])
-    mirror = lax.ppermute(own, ROW, [(i, 31 - i) for i in range(32)])
-    mirror_after = lax.ppermute(own, ROW, [(i, (32 - i) % 32) for i in range(32)])
+    half = lax.dynamic_slice_in_dim(own, BLOCK // 2 * lax.axis_index("core"), BLOCK // 2, 0)
+    after = lax.ppermute(half, ROW, [(i, (i - 1) % 32) for i in range(32)])
+    mirror = lax.ppermute(half, ROW, [(i, 31 - i) for i in range(32)])
+    mirror_after = lax.ppermute(half, ROW, [(i, (32 - i) % 32) for i in range(32)])
     pieces = sent_to_all(piece, ROW)
+    mine = jnp.stack([after, mirror, mirror_after])
+    other = lax.ppermute(mine, "core", CORES_SWAPPED)
     every_offset = pieces[:16, 16, :3].astype(jnp.int32)
     place = jnp.stack([r, c]).astype(jnp.int32)
     cov, cov_near, mapped = covariance_block(
-        place, every_offset, own, after, mirror, mirror_after, tail, pieces, start_basis
+        place, every_offset, own, mine, other, tail, pieces, start_basis
     )
     mapped = total_over(mapped, ROW)
     half = (3 * K // 4, BLOCK)
     kept, sent = local_call(image_kernel, [half, half], place, mapped, cov_near)
-    swap = [(0, 1), (1, 0)]
-    mine = sent_to_all(kept + lax.ppermute(sent, "core", swap), "z").sum(axis=0)
-    other = lax.ppermute(mine, "core", swap)
+    mine = sent_to_all(kept + lax.ppermute(sent, "core", CORES_SWAPPED), "z").sum(axis=0)
+    other = lax.ppermute(mine, "core", CORES_SWAPPED)
     mapped, grams = local_call(
         first_factor_kernel, [(K, BLOCK), (4, K // 2, 2 * K)], place, mine, other
     )

time: 137 us -> 139 us (1.015)
  starting transfers between devices: 45 us -> 46.9 us
    ppermute x5 -> x6, starting transfers between devices: 22.7 us -> 24.7 us  [the longest x2 9.62 us: per_device(): other = lax.ppermute(mine, 'core', CORES_SWAPPED)]
    all_to_all x1, waiting for transfers between devices: 1.55 us -> 0.01 us  [sent_to_all(): return lax.all_to_all(copies, axis, split_axis=0, concat_axis=0, tiled=True)]
    ppermute x5 -> x6, waiting for transfers between devices: 5.38 us -> 6.53 us  [the longest x1 4.08 us: per_device(): mirror = lax.ppermute(half, ROW, [(i, 31 - i) for i in range(32)])]
  transfers between devices with their start and end apart: 7 -> 8, of which waited for: 5 -> 6; matrix products, arithmetic and copies ran while one was open for 1% -> 1% of each run, Pallas kernels for 0% -> 0%
where the time goes in v3:
time: 139 us; the launch traced here: 138 us
  blocking collectives  68.5 us (49%)
  starting transfers between devices  46.9 us (34%)
  Pallas kernels  11.3 us (8%)
  waiting for transfers between devices  7.38 us (5%)
  local copies, waits for them, and re-layouts  2.36 us (2%)
    all_to_all x3, blocking collectives, sent_to_all(): return lax.all_to_all(copies, axis, split_axis=0, concat_axis=0, tiled=True)  42.4 us
    all_to_all x2, blocking collectives, exchanged(): return lax.all_to_all(tiles, axis, split_axis=0, concat_axis=0, tiled=True)  26.1 us
    ppermute x1, starting transfers between devices, per_device(): piece = lax.ppermute(piece, EVERY, piece_routes())  15 us
    ppermute x2, starting transfers between devices, per_device(): other = lax.ppermute(mine, 'core', CORES_SWAPPED)  9.62 us
    all_to_all x1, starting transfers between devices, sent_to_all(): return lax.all_to_all(copies, axis, split_axis=0, concat_axis=0, tiled=True)  7.15 us
    ppermute x1, starting transfers between devices, per_device(): after = lax.ppermute(half, ROW, [(i, (i - 1) % 32) for i in range(32)])  6.55 us
    pallas_call x3, Pallas kernels, local_call(): pl.pallas_call(kernel, in_specs=[pl.BlockSpec(memory_space=space) for spa...  6.16 us
    pallas_call x1, Pallas kernels, covariance_block(): pl.pallas_call(covariance_kernel, name='covariance_block', in_specs=[pl.B...  5.09 us
  transfers between devices with their start and end apart: 8, of which 6 were waited for; matrix products, arithmetic and copies ran while one was open for 1% of the time, Pallas kernels for 0%

profile of v3, /device:TPU:1, one launch (start us, length us, event | category | flops | bytes accessed | tf_op | source)
XLA Modules:
  0.0 138.5 jit_solution(10319946051124562109)
XLA Ops:
  0.6 0.0 copy-start.1
  0.7 0.8 copy-done.1
  1.5 0.0 copy-start.3
  1.5 0.6 copy-done.3
  2.1 15.0 %collective-permute-start = (bf16[32,256]{1,0:T(8,128)(2,1)S(1)}, bf16[32,256]{1,0:T(8,128)(2,1)S(1)}, u32[]{:S(2)}, u32[]{:S(2)}) collective-permute-start(bf16[32,256]{1,0:T(8,128)(2,1)S(1)} %fusion.2), channel_id=1, source_target_pairs={{0,256},{1,287},{2,303},{3,304},{4,320},{5,351},{6,367},{7,368},{8... | collective-permute-start | bytes 49160 | tf_op jit(solution)/shard_map/ppermute | solution.py:254
  17.1 0.8 collective-permute-done
  18.0 0.8 broadcast_in_dim.17
  18.8 7.2 %all-to-all-start = ((bf16[32,32,256]{2,1,0:T(8,128)(2,1)}), bf16[32,32,256]{2,1,0:T(8,128)(2,1)S(1)}, u32[]{:S(2)}, u32[]{:S(2)}) async-start(bf16[32,32,256]{2,1,0:T(8,128)(2,1)} %broadcast_in_dim.17), calls=%async_computation | async-start | bytes 1048576 | tf_op jit(solution)/shard_map/all_to_all | solution.py:41
  26.0 0.0 copy-start.2
  26.0 6.6 %collective-permute-start.1 = (bf16[64,256]{1,0:T(8,128)(2,1)S(1)}, bf16[64,256]{1,0:T(8,128)(2,1)S(1)}, u32[]{:S(2)}, u32[]{:S(2)}) collective-permute-start(bf16[64,256]{1,0:T(8,128)(2,1)S(1)} %constant_dynamic-slice_fusion), channel_id=1, source_target_pairs={{0,496},{16,0},{32,16},{48,32},{64,48},{80,64},{96,80},{112,96},{1... | collective-permute-start | bytes 98312 | tf_op jit(solution)/shard_map/ppermute | solution.py:256
  32.6 3.1 %collective-permute-start.2 = (bf16[64,256]{1,0:T(8,128)(2,1)S(1)}, bf16[64,256]{1,0:T(8,128)(2,1)S(1)}, u32[]{:S(2)}, u32[]{:S(2)}) collective-permute-start(bf16[64,256]{1,0:T(8,128)(2,1)S(1)} %constant_dynamic-slice_fusion), channel_id=1, source_target_pairs={{0,496},{16,480},{32,464},{48,448},{64,432},{80,416},{96,400},{112... | collective-permute-start | bytes 98312 | tf_op jit(solution)/shard_map/ppermute | solution.py:257
  35.7 0.7 collective-permute-start.3
  36.3 0.6 pad_add_fusion.place
  36.9 0.0 copy-done.2
  36.9 0.5 collective-permute-done.1
  37.4 4.1 %collective-permute-done.2 = bf16[64,256]{1,0:T(8,128)(2,1)S(1)} collective-permute-done((bf16[64,256]{1,0:T(8,128)(2,1)S(1)}, bf16[64,256]{1,0:T(8,128)(2,1)S(1)}, u32[]{:S(2)}, u32[]{:S(2)}) %collective-permute-start.2) | collective-permute-done | bytes 32800 | tf_op jit(solution)/shard_map/ppermute | solution.py:257
  41.5 0.0 collective-permute-done.3
  41.5 0.0 copy-start
  41.5 5.7 %collective-permute-start.4 = (bf16[3,64,256]{2,1,0:T(8,128)(2,1)S(1)}, bf16[3,64,256]{2,1,0:T(8,128)(2,1)S(1)}, u32[]{:S(2)}, u32[]{:S(2)}) collective-permute-start(bf16[3,64,256]{2,1,0:T(8,128)(2,1)S(1)} %pad_maximum_fusion.mine), channel_id=1, source_target_pairs={{0,1},{1,0},{2,3},{3,2},{4,5},{5,4},{6,7},{7,6},{8,9},{9,8},{10,11... | collective-permute-start | bytes 294920 | tf_op jit(solution)/shard_map/ppermute | solution.py:261
  47.3 0.0 all-to-all-done.pieces
  47.3 0.6 slice_convert_fusion
  47.9 0.3 collective-permute-done.4.other
  48.2 0.0 copy-done
  48.2 5.1 %covariance_block.1 = (f32[128,256]{1,0:T(8,128)}, f32[128,256]{1,0:T(8,128)S(1)}, f32[32,4,128]{2,1,0:T(4,128)S(1)}) custom-call(s32[2]{0:T(128)} %pad_add_fusion.place, s32[16,3]{1,0:T(8,128)} %bitcast.23, bf16[128,256]{1,0:T(8,128)(2,1)S(1)} %bitcast.19, bf16[3,64,256]{2,1,0:T(8,128)(2,1)S(1)} %pad_maximum_fusion.mine, ...), custom_call_target="tpu_custom_call" | custom-call | tf_op jit(solution)/shard_map/covariance_block/pallas_call | solution.py:121
  53.3 19.2 %all_to_all.30 = f32[32,4,128]{2,1,0:T(4,128)S(1)} all-to-all(f32[32,4,128]{2,1,0:T(4,128)S(1)} %get-tuple-element.10), channel_id=1, replica_groups=mesh['row_0'=4,'row_1'=8,'z'=8,'core'=2] {'row_0','row_1'}, dimensions={0} | all-to-all | bytes 131072 | tf_op jit(solution)/shard_map/all_to_all | solution.py:223
  72.6 11.9 %all_to_all.31.mapped = f32[32,4,128]{2,1,0:T(4,128)S(1)} all-to-all(f32[32,4,128]{2,1,0:T(4,128)S(1)} %broadcast_in_dim.18), channel_id=1, replica_groups=mesh['row_0'=4,'row_1'=8,'z'=8,'core'=2] {'row_0','row_1'}, dimensions={0} | all-to-all | bytes 131072 | tf_op jit(solution)/shard_map/all_to_all | solution.py:41
  84.5 1.0 shard_map.59
  85.5 4.8 %collective-permute-start.5 = (f32[48,128]{1,0:T(8,128)S(1)}, f32[48,128]{1,0:T(8,128)S(1)}, u32[]{:S(2)}, u32[]{:S(2)}) collective-permute-start(f32[48,128]{1,0:T(8,128)S(1)} %get-tuple-element.13), channel_id=1, source_target_pairs={{0,1},{1,0},{2,3},{3,2},{4,5},{5,4},{6,7},{7,6},{8,9},{9,8},{10,11... | collective-permute-start | bytes 73736 | tf_op jit(solution)/shard_map/ppermute | solution.py:270
  90.3 0.8 collective-permute-done.5
  91.2 20.1 %all_to_all.32 = f32[8,48,128]{2,1,0:T(8,128)S(1)} all-to-all(f32[8,48,128]{2,1,0:T(8,128)S(1)} %broadcast_in_dim.19), channel_id=1, replica_groups=mesh['row_0'=4,'row_1'=8,'z'=8,'core'=2] {'z'}, dimensions={0} | all-to-all | bytes 393216 | tf_op jit(solution)/shard_map/all_to_all | solution.py:41
  111.4 3.9 %collective-permute-start.6 = (f32[48,128]{1,0:T(8,128)S(1)}, f32[48,128]{1,0:T(8,128)S(1)}, u32[]{:S(2)}, u32[]{:S(2)}) collective-permute-start(f32[48,128]{1,0:T(8,128)S(1)} %reduce_sum.28.mine), channel_id=1, source_target_pairs={{0,1},{1,0},{2,3},{3,2},{4,5},{5,4},{6,7},{7,6},{8,9},{9,8},{10,11... | collective-permute-start | bytes 73736 | tf_op jit(solution)/shard_map/ppermute | solution.py:271
  115.2 0.8 collective-permute-done.6.other
  116.1 2.7 %shard_map.60 = (f32[64,128]{1,0:T(8,128)S(1)}, f32[4,32,128]{2,1,0:T(8,128)S(1)}) custom-call(s32[2]{0:T(128)} %pad_add_fusion.place, f32[48,128]{1,0:T(8,128)S(1)} %reduce_sum.28.mine, f32[48,128]{1,0:T(8,128)S(1)} %collective-permute-done.6.other), custom_call_target="tpu_custom_call" | custom-call | tf_op jit(solution)/shard_map/pallas_call | solution.py:215
  118.8 6.9 %all_to_all.33 = f32[4,32,128]{2,1,0:T(8,128)S(1)} all-to-all(f32[4,32,128]{2,1,0:T(8,128)S(1)} %get-tuple-element.14), channel_id=1, replica_groups=mesh['row_0'=4,'row_1'=8,'z'=8,'core'=2] {'row_0'}, dimensions={0} | all-to-all | bytes 131072 | tf_op jit(solution)/shard_map/all_to_all | solution.py:223
  125.7 10.3 %all_to_all.34.grams = f32[8,32,128]{2,1,0:T(8,128)S(1)} all-to-all(f32[8,32,128]{2,1,0:T(8,128)S(1)} %broadcast_in_dim.20), channel_id=1, replica_groups=mesh['row_0'=4,'row_1'=8,'z'=8,'core'=2] {'row_1'}, dimensions={0} | all-to-all | bytes 262144 | tf_op jit(solution)/shard_map/all_to_all | solution.py:41
  136.0 2.4 %shard_map.61 = f32[64,128]{1,0:T(8,128)} custom-call(f32[8,32,128]{2,1,0:T(8,128)S(1)} %all_to_all.34.grams, f32[64,128]{1,0:T(8,128)S(1)} %get-tuple-element.15.mapped), custom_call_target="tpu_custom_call" | custom-call | tf_op jit(solution)/shard_map/pallas_call | solution.py:215
  (14 shorter events, 0.2 us)
Async XLA Ops:
  0.6 0.8 copy-start.1
  1.5 0.7 copy-start.3
  2.1 15.8 %collective-permute-start = (bf16[32,256]{1,0:T(8,128)(2,1)S(1)}, bf16[32,256]{1,0:T(8,128)(2,1)S(1)}, u32[]{:S(2)}, u32[]{:S(2)}) collective-permute-start(bf16[32,256]{1,0:T(8,128)(2,1)S(1)} %fusion.2), channel_id=1, source_target_pairs={{0,256},{1,287},{2,303},{3,304},{4,320},{5,351},{6,367},{7,368},{8... | collective-permute-start | bytes 49160 | tf_op jit(solution)/shard_map/ppermute | solution.py:254
  18.8 28.5 %all-to-all-start = ((bf16[32,32,256]{2,1,0:T(8,128)(2,1)}), bf16[32,32,256]{2,1,0:T(8,128)(2,1)S(1)}, u32[]{:S(2)}, u32[]{:S(2)}) async-start(bf16[32,32,256]{2,1,0:T(8,128)(2,1)} %broadcast_in_dim.17), calls=%async_computation | async-start | bytes 1048576 | tf_op jit(solution)/shard_map/all_to_all | solution.py:41
  26.0 11.0 %copy-start.2 = (bf16[128,2,128]{2,1,0:T(2,128)(2,1)S(1)}, bf16[128,2,128]{2,1,0:T(2,128)(2,1)}, u32[]{:S(2)}) copy-start(bf16[128,2,128]{2,1,0:T(2,128)(2,1)} %param.5) | copy-start | bytes 196612
  26.0 11.4 %collective-permute-start.1 = (bf16[64,256]{1,0:T(8,128)(2,1)S(1)}, bf16[64,256]{1,0:T(8,128)(2,1)S(1)}, u32[]{:S(2)}, u32[]{:S(2)}) collective-permute-start(bf16[64,256]{1,0:T(8,128)(2,1)S(1)} %constant_dynamic-slice_fusion), channel_id=1, source_target_pairs={{0,496},{16,0},{32,16},{48,32},{64,48},{80,64},{96,80},{112,96},{1... | collective-permute-start | bytes 98312 | tf_op jit(solution)/shard_map/ppermute | solution.py:256
  32.6 9.0 %collective-permute-start.2 = (bf16[64,256]{1,0:T(8,128)(2,1)S(1)}, bf16[64,256]{1,0:T(8,128)(2,1)S(1)}, u32[]{:S(2)}, u32[]{:S(2)}) collective-permute-start(bf16[64,256]{1,0:T(8,128)(2,1)S(1)} %constant_dynamic-slice_fusion), channel_id=1, source_target_pairs={{0,496},{16,480},{32,464},{48,448},{64,432},{80,416},{96,400},{112... | collective-permute-start | bytes 98312 | tf_op jit(solution)/shard_map/ppermute | solution.py:257
  35.7 5.9 %collective-permute-start.3 = (bf16[64,256]{1,0:T(8,128)(2,1)S(1)}, bf16[64,256]{1,0:T(8,128)(2,1)S(1)}, u32[]{:S(2)}, u32[]{:S(2)}) collective-permute-start(bf16[64,256]{1,0:T(8,128)(2,1)S(1)} %constant_dynamic-slice_fusion), channel_id=1, source_target_pairs={{0,0},{16,496},{32,480},{48,464},{64,448},{80,432},{96,416},{112,4... | collective-permute-start | bytes 98312 | tf_op jit(solution)/shard_map/ppermute | solution.py:258
  41.5 6.7 %copy-start = (f32[64,128]{1,0:T(8,128)S(1)}, f32[64,128]{1,0:T(8,128)}, u32[]{:S(2)}) copy-start(f32[64,128]{1,0:T(8,128)} %basis.1) | copy-start | bytes 98308
  41.5 6.7 %collective-permute-start.4 = (bf16[3,64,256]{2,1,0:T(8,128)(2,1)S(1)}, bf16[3,64,256]{2,1,0:T(8,128)(2,1)S(1)}, u32[]{:S(2)}, u32[]{:S(2)}) collective-permute-start(bf16[3,64,256]{2,1,0:T(8,128)(2,1)S(1)} %pad_maximum_fusion.mine), channel_id=1, source_target_pairs={{0,1},{1,0},{2,3},{3,2},{4,5},{5,4},{6,7},{7,6},{8,9},{9,8},{10,11... | collective-permute-start | bytes 294920 | tf_op jit(solution)/shard_map/ppermute | solution.py:261
  85.5 5.7 %collective-permute-start.5 = (f32[48,128]{1,0:T(8,128)S(1)}, f32[48,128]{1,0:T(8,128)S(1)}, u32[]{:S(2)}, u32[]{:S(2)}) collective-permute-start(f32[48,128]{1,0:T(8,128)S(1)} %get-tuple-element.13), channel_id=1, source_target_pairs={{0,1},{1,0},{2,3},{3,2},{4,5},{5,4},{6,7},{7,6},{8,9},{9,8},{10,11... | collective-permute-start | bytes 73736 | tf_op jit(solution)/shard_map/ppermute | solution.py:270
  111.4 4.7 %collective-permute-start.6 = (f32[48,128]{1,0:T(8,128)S(1)}, f32[48,128]{1,0:T(8,128)S(1)}, u32[]{:S(2)}, u32[]{:S(2)}) collective-permute-start(f32[48,128]{1,0:T(8,128)S(1)} %reduce_sum.28.mine), channel_id=1, source_target_pairs={{0,1},{1,0},{2,3},{3,2},{4,5},{5,4},{6,7},{7,6},{8,9},{9,8},{10,11... | collective-permute-start | bytes 73736 | tf_op jit(solution)/shard_map/ppermute | solution.py:271

commit v4 on v1

--- a/solution.py
+++ b/solution.py
@@ -104,8 +104,8 @@
     cov[...] = block
     cov_near[...] = block
     image = dot_nn(basis[...], block, HIGH)
-    for p in range(32):
-        mapped[p] = image[4 * (p // 2) : 4 * (p // 2) + 4, SNAPS * (p % 2) : SNAPS * (p % 2) + SNAPS]
+    for t in range(8):
+        mapped[t] = image[8 * t : 8 * t + 8]
 
 
 def covariance_block(place, offsets, own, after, mirror, mirror_after, tail, pieces, basis):
@@ -118,7 +118,7 @@
         out_shape=[
             jax.ShapeDtypeStruct((BLOCK, 2 * BLOCK), jnp.float32),
             pltpu.VMEM((BLOCK, 2 * BLOCK), jnp.float32),
-            pltpu.VMEM((32, 4, SNAPS), jnp.float32),
+            pltpu.VMEM((8, 8, 2 * BLOCK), jnp.float32),
         ],
         scratch_shapes=[
             pltpu.VMEM((2, 2 * BLOCK, SNAPS), jnp.float32),
@@ -165,9 +165,7 @@
 
 
 def image_kernel(place, mapped, cov, kept, sent):
-    image = jnp.concatenate(
-        [jnp.concatenate([mapped[2 * i], mapped[2 * i + 1]], axis=1) for i in range(16)], axis=0
-    )
+    image = jnp.concatenate([mapped[t] for t in range(8)], axis=0)
     product = dot_nt(image, cov[...], HIGH)
     gram = dot_nt(image, image, HIGH)
     terms = jnp.concatenate([product, halves_side_by_side(gram)], axis=0)
@@ -181,6 +179,27 @@
     return jnp.concatenate([gram[: K // 2], gram[K // 2 :]], axis=1)
 
 
+def distinct_blocks(gram):
+    h = K // 2
+    wide = jnp.concatenate([gram[:h, :h], gram[h:, :h], gram[h:, h:]], axis=1)
+    return jnp.concatenate(
+        [
+            jnp.concatenate([wide[8 * i : 8 * i + 8], wide[24:, h * i : h * i + h]], axis=1)
+            for i in range(3)
+        ],
+        axis=0,
+    )
+
+
+def from_distinct_blocks(packed):
+    h = K // 2
+    last = jnp.concatenate([packed[8 * i : 8 * i + 8, 3 * h :] for i in range(3)], axis=1)
+    wide = jnp.concatenate([packed[:, : 3 * h], last], axis=0)
+    low = wide[:, h : 2 * h]
+    top = jnp.concatenate([wide[:, :h], low.T], axis=1)
+    return jnp.concatenate([top, jnp.concatenate([low, wide[:, 2 * h :]], axis=1)], axis=0)
+
+
 def halves_stacked(packed):
     return jnp.concatenate([packed[:, :K], packed[:, K:]], axis=0)
 
@@ -192,14 +211,14 @@
     )
     image = dot_nn(inverse_factor(halves_stacked(total[K:])), total[:K], HIGH)
     mapped[...] = image
-    part = halves_side_by_side(dot_nt(image, image, HIGH))
+    part = distinct_blocks(dot_nt(image, image, HIGH))
     for i in range(grams.shape[0]):
         grams[i] = part
 
 
 def last_factor_kernel(grams, mapped, basis):
     total = jnp.sum(grams[...], axis=0)
-    basis[...] = dot_nn(inverse_factor(halves_stacked(total)), mapped[...], HIGH)
+    basis[...] = dot_nn(inverse_factor(from_distinct_blocks(total)), mapped[...], HIGH)
 
 
 def local_call(kernel, shapes, *operands, result=pltpu.VMEM):
@@ -213,10 +232,6 @@
 
 def exchanged(tiles, axis):
     return lax.all_to_all(tiles, axis, split_axis=0, concat_axis=0, tiled=True)
-
-
-def total_over(tiles, axis):
-    return sent_to_all(exchanged(tiles, axis).sum(axis=0), axis)
 
 
 def piece_routes():
@@ -253,14 +268,15 @@
     cov, cov_near, mapped = covariance_block(
         place, every_offset, own, after, mirror, mirror_after, tail, pieces, start_basis
     )
-    mapped = total_over(mapped, ROW)
+    mapped = exchanged(mapped, "row_1").sum(axis=0)
+    mapped = sent_to_all(sent_to_all(mapped, "row_0").sum(axis=0), "row_1")
     half = (3 * K // 4, BLOCK)
     kept, sent = local_call(image_kernel, [half, half], place, mapped, cov_near)
     swap = [(0, 1), (1, 0)]
     mine = sent_to_all(kept + lax.ppermute(sent, "core", swap), "z").sum(axis=0)
     other = lax.ppermute(mine, "core", swap)
     mapped, grams = local_call(
-        first_factor_kernel, [(K, BLOCK), (4, K // 2, 2 * K)], place, mine, other
+        first_factor_kernel, [(K, BLOCK), (4, 3 * K // 8, 2 * K)], place, mine, other
     )
     grams = sent_to_all(exchanged(grams, "row_0").sum(axis=0), "row_1")
     (basis,) = local_call(last_factor_kernel, [(K, BLOCK)], grams, mapped, result=jax.ShapeDtypeStruct)

time: 137 us -> 140 us (1.022)
  blocking collectives: 67.3 us -> 68.7 us
    all_to_all x3 -> x4, blocking collectives: 42.3 us -> 46.4 us  [sent_to_all(): return lax.all_to_all(copies, axis, split_axis=0, concat_axis=0, tiled=True)]
    all_to_all x2, blocking collectives: 25 us -> 22.3 us  [exchanged(): return lax.all_to_all(tiles, axis, split_axis=0, concat_axis=0, tiled=True)]
    ppermute x1, starting transfers between devices: 8.55 us -> 10 us  [per_device(): mine = sent_to_all(kept + lax.ppermute(sent, 'core', swap), 'z').sum(axis=0)]
where the time goes in v4:
time: 140 us; the launch traced here: 139 us
  blocking collectives  68.7 us (49%)
  starting transfers between devices  46.4 us (33%)
  Pallas kernels  11.6 us (8%)
  waiting for transfers between devices  7.78 us (6%)
  local copies, waits for them, and re-layouts  2.35 us (2%)
    all_to_all x4, blocking collectives, sent_to_all(): return lax.all_to_all(copies, axis, split_axis=0, concat_axis=0, tiled=True)  46.4 us
    all_to_all x2, blocking collectives, exchanged(): return lax.all_to_all(tiles, axis, split_axis=0, concat_axis=0, tiled=True)  22.3 us
    ppermute x1, starting transfers between devices, per_device(): piece = lax.ppermute(piece, EVERY, piece_routes())  15 us
    ppermute x1, starting transfers between devices, per_device(): mine = sent_to_all(kept + lax.ppermute(sent, 'core', swap), 'z').sum(axis=0)  10 us
    all_to_all x1, starting transfers between devices, sent_to_all(): return lax.all_to_all(copies, axis, split_axis=0, concat_axis=0, tiled=True)  7.28 us
    ppermute x1, starting transfers between devices, per_device(): after = lax.ppermute(own, ROW, [(i, (i - 1) % 32) for i in range(32)])  6.55 us
    pallas_call x3, Pallas kernels, local_call(): pl.pallas_call(kernel, in_specs=[pl.BlockSpec(memory_space=space) for spa...  6.54 us
    pallas_call x1, Pallas kernels, covariance_block(): pl.pallas_call(covariance_kernel, name='covariance_block', in_specs=[pl.B...  5.09 us
  transfers between devices with their start and end apart: 7, of which 5 were waited for; matrix products, arithmetic and copies ran while one was open for 1% of the time, Pallas kernels for 0%

profile of v4, /device:TPU:1, one launch (start us, length us, event | category | flops | bytes accessed | tf_op | source)
XLA Modules:
  0.0 139.0 jit_solution(7415897668885997081)
XLA Ops:
  0.6 0.0 copy-start.1
  0.7 0.8 copy-done.1
  1.5 0.0 copy-start.3
  1.5 0.6 copy-done.3
  2.1 15.0 %collective-permute-start = (bf16[32,256]{1,0:T(8,128)(2,1)S(1)}, bf16[32,256]{1,0:T(8,128)(2,1)S(1)}, u32[]{:S(2)}, u32[]{:S(2)}) collective-permute-start(bf16[32,256]{1,0:T(8,128)(2,1)S(1)} %fusion.2), channel_id=1, source_target_pairs={{0,256},{1,287},{2,303},{3,304},{4,320},{5,351},{6,367},{7,368},{8... | collective-permute-start | bytes 49160 | tf_op jit(solution)/shard_map/ppermute | solution.py:261
  17.1 0.8 collective-permute-done
  18.0 0.8 broadcast_in_dim.20
  18.8 0.0 copy-start.2
  18.8 7.3 %all-to-all-start = ((bf16[32,32,256]{2,1,0:T(8,128)(2,1)}), bf16[32,32,256]{2,1,0:T(8,128)(2,1)S(1)}, u32[]{:S(2)}, u32[]{:S(2)}) async-start(bf16[32,32,256]{2,1,0:T(8,128)(2,1)} %broadcast_in_dim.20), calls=%async_computation | async-start | bytes 1048576 | tf_op jit(solution)/shard_map/all_to_all | solution.py:40
  26.1 6.6 %collective-permute-start.1 = (bf16[128,256]{1,0:T(8,128)(2,1)S(1)}, bf16[128,256]{1,0:T(8,128)(2,1)S(1)}, u32[]{:S(2)}, u32[]{:S(2)}) collective-permute-start(bf16[128,256]{1,0:T(8,128)(2,1)S(1)} %bitcast.15), channel_id=1, source_target_pairs={{0,496},{16,0},{32,16},{48,32},{64,48},{80,64},{96,80},{112,96},{1... | collective-permute-start | bytes 196616 | tf_op jit(solution)/shard_map/ppermute | solution.py:262
  32.7 3.1 %collective-permute-start.2 = (bf16[128,256]{1,0:T(8,128)(2,1)S(1)}, bf16[128,256]{1,0:T(8,128)(2,1)S(1)}, u32[]{:S(2)}, u32[]{:S(2)}) collective-permute-start(bf16[128,256]{1,0:T(8,128)(2,1)S(1)} %bitcast.16), channel_id=1, source_target_pairs={{0,496},{16,480},{32,464},{48,448},{64,432},{80,416},{96,400},{112... | collective-permute-start | bytes 196616 | tf_op jit(solution)/shard_map/ppermute | solution.py:263
  35.7 0.7 collective-permute-start.3
  36.4 0.0 copy-done.2
  36.4 0.0 copy-start
  36.5 0.6 pad_add_fusion.place
  37.0 1.6 %all-to-all-done.pieces = bf16[32,32,256]{2,1,0:T(8,128)(2,1)S(1)} async-done(((bf16[32,32,256]{2,1,0:T(8,128)(2,1)}), bf16[32,32,256]{2,1,0:T(8,128)(2,1)S(1)}, u32[]{:S(2)}, u32[]{:S(2)}) %all-to-all-start) | async-done | bytes 524320 | tf_op jit(solution)/shard_map/all_to_all | solution.py:40
  38.6 0.6 slice_convert_fusion
  39.2 0.0 collective-permute-done.1.after
  39.2 3.7 %collective-permute-done.2.mirror = bf16[128,256]{1,0:T(8,128)(2,1)S(1)} collective-permute-done((bf16[128,256]{1,0:T(8,128)(2,1)S(1)}, bf16[128,256]{1,0:T(8,128)(2,1)S(1)}, u32[]{:S(2)}, u32[]{:S(2)}) %collective-permute-start.2) | collective-permute-done | bytes 65568 | tf_op jit(solution)/shard_map/ppermute | solution.py:263
  42.9 0.0 collective-permute-done.3.mirror_after
  42.9 0.0 copy-done
  42.9 5.1 %covariance_block.1 = (f32[128,256]{1,0:T(8,128)}, f32[128,256]{1,0:T(8,128)S(1)}, f32[8,8,256]{2,1,0:T(8,128)S(1)}) custom-call(s32[2]{0:T(128)} %pad_add_fusion.place, s32[16,3]{1,0:T(8,128)} %bitcast.22, bf16[128,256]{1,0:T(8,128)(2,1)S(1)} %bitcast.18, bf16[128,256]{1,0:T(8,128)(2,1)S(1)} %collective-permute-done.1.after, ...), custom_call_target="tpu_custom_call" | custom-call | tf_op jit(solution)/shard_map/covariance_block/pallas_call | solution.py:113
  48.0 15.6 %all_to_all.35 = f32[8,8,256]{2,1,0:T(8,128)S(1)} all-to-all(f32[8,8,256]{2,1,0:T(8,128)S(1)} %get-tuple-element.10), channel_id=1, replica_groups=mesh['row_0'=4,'row_1'=8,'z'=8,'core'=2] {'row_1'}, dimensions={0} | all-to-all | bytes 131072 | tf_op jit(solution)/shard_map/all_to_all | solution.py:234
  63.6 6.7 %all_to_all.36 = f32[4,8,256]{2,1,0:T(8,128)S(1)} all-to-all(f32[4,8,256]{2,1,0:T(8,128)S(1)} %broadcast_in_dim.21), channel_id=1, replica_groups=mesh['row_0'=4,'row_1'=8,'z'=8,'core'=2] {'row_0'}, dimensions={0} | all-to-all | bytes 65536 | tf_op jit(solution)/shard_map/all_to_all | solution.py:40
  70.3 9.6 %all_to_all.37.mapped = f32[8,8,256]{2,1,0:T(8,128)S(1)} all-to-all(f32[8,8,256]{2,1,0:T(8,128)S(1)} %broadcast_in_dim.22), channel_id=1, replica_groups=mesh['row_0'=4,'row_1'=8,'z'=8,'core'=2] {'row_1'}, dimensions={0} | all-to-all | bytes 131072 | tf_op jit(solution)/shard_map/all_to_all | solution.py:40
  79.9 1.0 shard_map.59
  80.9 10.0 %collective-permute-start.4 = (f32[48,128]{1,0:T(8,128)S(1)}, f32[48,128]{1,0:T(8,128)S(1)}, u32[]{:S(2)}, u32[]{:S(2)}) collective-permute-start(f32[48,128]{1,0:T(8,128)S(1)} %get-tuple-element.13), channel_id=1, source_target_pairs={{0,1},{1,0},{2,3},{3,2},{4,5},{5,4},{6,7},{7,6},{8,9},{9,8},{10,11... | collective-permute-start | bytes 73736 | tf_op jit(solution)/shard_map/ppermute | solution.py:276
  90.9 0.8 collective-permute-done.4
  91.8 20.1 %all_to_all.38 = f32[8,48,128]{2,1,0:T(8,128)S(1)} all-to-all(f32[8,48,128]{2,1,0:T(8,128)S(1)} %broadcast_in_dim.23), channel_id=1, replica_groups=mesh['row_0'=4,'row_1'=8,'z'=8,'core'=2] {'z'}, dimensions={0} | all-to-all | bytes 393216 | tf_op jit(solution)/shard_map/all_to_all | solution.py:40
  111.9 3.9 %collective-permute-start.5 = (f32[48,128]{1,0:T(8,128)S(1)}, f32[48,128]{1,0:T(8,128)S(1)}, u32[]{:S(2)}, u32[]{:S(2)}) collective-permute-start(f32[48,128]{1,0:T(8,128)S(1)} %reduce_sum.38.mine), channel_id=1, source_target_pairs={{0,1},{1,0},{2,3},{3,2},{4,5},{5,4},{6,7},{7,6},{8,9},{9,8},{10,11... | collective-permute-start | bytes 73736 | tf_op jit(solution)/shard_map/ppermute | solution.py:277
  115.8 0.8 collective-permute-done.5.other
  116.7 2.8 %shard_map.60 = (f32[64,128]{1,0:T(8,128)S(1)}, f32[4,24,128]{2,1,0:T(8,128)S(1)}) custom-call(s32[2]{0:T(128)} %pad_add_fusion.place, f32[48,128]{1,0:T(8,128)S(1)} %reduce_sum.38.mine, f32[48,128]{1,0:T(8,128)S(1)} %collective-permute-done.5.other), custom_call_target="tpu_custom_call" | custom-call | tf_op jit(solution)/shard_map/pallas_call | solution.py:226
  119.5 6.8 %all_to_all.39 = f32[4,24,128]{2,1,0:T(8,128)S(1)} all-to-all(f32[4,24,128]{2,1,0:T(8,128)S(1)} %get-tuple-element.14), channel_id=1, replica_groups=mesh['row_0'=4,'row_1'=8,'z'=8,'core'=2] {'row_0'}, dimensions={0} | all-to-all | bytes 98304 | tf_op jit(solution)/shard_map/all_to_all | solution.py:234
  126.3 10.0 %all_to_all.40.grams = f32[8,24,128]{2,1,0:T(8,128)S(1)} all-to-all(f32[8,24,128]{2,1,0:T(8,128)S(1)} %broadcast_in_dim.24), channel_id=1, replica_groups=mesh['row_0'=4,'row_1'=8,'z'=8,'core'=2] {'row_1'}, dimensions={0} | all-to-all | bytes 196608 | tf_op jit(solution)/shard_map/all_to_all | solution.py:40
  136.2 2.7 %shard_map.61 = f32[64,128]{1,0:T(8,128)} custom-call(f32[8,24,128]{2,1,0:T(8,128)S(1)} %all_to_all.40.grams, f32[64,128]{1,0:T(8,128)S(1)} %get-tuple-element.15.mapped), custom_call_target="tpu_custom_call" | custom-call | tf_op jit(solution)/shard_map/pallas_call | solution.py:226
  (14 shorter events, 0.1 us)
Async XLA Ops:
  0.6 0.8 copy-start.1
  1.5 0.7 copy-start.3
  2.1 15.8 %collective-permute-start = (bf16[32,256]{1,0:T(8,128)(2,1)S(1)}, bf16[32,256]{1,0:T(8,128)(2,1)S(1)}, u32[]{:S(2)}, u32[]{:S(2)}) collective-permute-start(bf16[32,256]{1,0:T(8,128)(2,1)S(1)} %fusion.2), channel_id=1, source_target_pairs={{0,256},{1,287},{2,303},{3,304},{4,320},{5,351},{6,367},{7,368},{8... | collective-permute-start | bytes 49160 | tf_op jit(solution)/shard_map/ppermute | solution.py:261
  18.8 17.6 %copy-start.2 = (bf16[128,2,128]{2,1,0:T(2,128)(2,1)S(1)}, bf16[128,2,128]{2,1,0:T(2,128)(2,1)}, u32[]{:S(2)}) copy-start(bf16[128,2,128]{2,1,0:T(2,128)(2,1)} %param.5) | copy-start | bytes 196612
  18.8 19.8 %all-to-all-start = ((bf16[32,32,256]{2,1,0:T(8,128)(2,1)}), bf16[32,32,256]{2,1,0:T(8,128)(2,1)S(1)}, u32[]{:S(2)}, u32[]{:S(2)}) async-start(bf16[32,32,256]{2,1,0:T(8,128)(2,1)} %broadcast_in_dim.20), calls=%async_computation | async-start | bytes 1048576 | tf_op jit(solution)/shard_map/all_to_all | solution.py:40
  26.1 13.1 %collective-permute-start.1 = (bf16[128,256]{1,0:T(8,128)(2,1)S(1)}, bf16[128,256]{1,0:T(8,128)(2,1)S(1)}, u32[]{:S(2)}, u32[]{:S(2)}) collective-permute-start(bf16[128,256]{1,0:T(8,128)(2,1)S(1)} %bitcast.15), channel_id=1, source_target_pairs={{0,496},{16,0},{32,16},{48,32},{64,48},{80,64},{96,80},{112,96},{1... | collective-permute-start | bytes 196616 | tf_op jit(solution)/shard_map/ppermute | solution.py:262
  32.7 10.3 %collective-permute-start.2 = (bf16[128,256]{1,0:T(8,128)(2,1)S(1)}, bf16[128,256]{1,0:T(8,128)(2,1)S(1)}, u32[]{:S(2)}, u32[]{:S(2)}) collective-permute-start(bf16[128,256]{1,0:T(8,128)(2,1)S(1)} %bitcast.16), channel_id=1, source_target_pairs={{0,496},{16,480},{32,464},{48,448},{64,432},{80,416},{96,400},{112... | collective-permute-start | bytes 196616 | tf_op jit(solution)/shard_map/ppermute | solution.py:263
  35.7 7.2 %collective-permute-start.3 = (bf16[128,256]{1,0:T(8,128)(2,1)S(1)}, bf16[128,256]{1,0:T(8,128)(2,1)S(1)}, u32[]{:S(2)}, u32[]{:S(2)}) collective-permute-start(bf16[128,256]{1,0:T(8,128)(2,1)S(1)} %bitcast.17), channel_id=1, source_target_pairs={{0,0},{16,496},{32,480},{48,464},{64,448},{80,432},{96,416},{112,4... | collective-permute-start | bytes 196616 | tf_op jit(solution)/shard_map/ppermute | solution.py:264
  36.4 6.5 %copy-start = (f32[64,128]{1,0:T(8,128)S(1)}, f32[64,128]{1,0:T(8,128)}, u32[]{:S(2)}) copy-start(f32[64,128]{1,0:T(8,128)} %basis.1) | copy-start | bytes 98308
  80.9 10.9 %collective-permute-start.4 = (f32[48,128]{1,0:T(8,128)S(1)}, f32[48,128]{1,0:T(8,128)S(1)}, u32[]{:S(2)}, u32[]{:S(2)}) collective-permute-start(f32[48,128]{1,0:T(8,128)S(1)} %get-tuple-element.13), channel_id=1, source_target_pairs={{0,1},{1,0},{2,3},{3,2},{4,5},{5,4},{6,7},{7,6},{8,9},{9,8},{10,11... | collective-permute-start | bytes 73736 | tf_op jit(solution)/shard_map/ppermute | solution.py:276
  111.9 4.7 %collective-permute-start.5 = (f32[48,128]{1,0:T(8,128)S(1)}, f32[48,128]{1,0:T(8,128)S(1)}, u32[]{:S(2)}, u32[]{:S(2)}) collective-permute-start(f32[48,128]{1,0:T(8,128)S(1)} %reduce_sum.38.mine), channel_id=1, source_target_pairs={{0,1},{1,0},{2,3},{3,2},{4,5},{5,4},{6,7},{7,6},{8,9},{9,8},{10,11... | collective-permute-start | bytes 73736 | tf_op jit(solution)/shard_map/ppermute | solution.py:277

commit v5 on v1

--- a/solution.py
+++ b/solution.py
@@ -164,17 +164,12 @@
     return jnp.concatenate(done, axis=0)[:, K:]
 
 
-def image_kernel(place, mapped, cov, kept, sent):
+def image_kernel(mapped, cov, terms):
     image = jnp.concatenate(
         [jnp.concatenate([mapped[2 * i], mapped[2 * i + 1]], axis=1) for i in range(16)], axis=0
     )
-    product = dot_nt(image, cov[...], HIGH)
-    gram = dot_nt(image, image, HIGH)
-    terms = jnp.concatenate([product, halves_side_by_side(gram)], axis=0)
-    half = terms.shape[0] // 2
-    first = place[1] % 2 == 0
-    kept[...] = jnp.where(first, terms[:half], terms[half:])
-    sent[...] = jnp.where(first, terms[half:], terms[:half])
+    terms[:K] = dot_nt(image, cov[...], HIGH)
+    terms[K:] = halves_side_by_side(dot_nt(image, image, HIGH))
 
 
 def halves_side_by_side(gram):
@@ -185,11 +180,7 @@
     return jnp.concatenate([packed[:, :K], packed[:, K:]], axis=0)
 
 
-def first_factor_kernel(place, mine, other, mapped, grams):
-    first = place[1] % 2 == 0
-    total = jnp.concatenate(
-        [jnp.where(first, mine[...], other[...]), jnp.where(first, other[...], mine[...])], axis=0
-    )
+def first_factor_kernel(total, mapped, grams):
     image = dot_nn(inverse_factor(halves_stacked(total[K:])), total[:K], HIGH)
     mapped[...] = image
     part = halves_side_by_side(dot_nt(image, image, HIGH))
@@ -254,14 +245,12 @@
         place, every_offset, own, after, mirror, mirror_after, tail, pieces, start_basis
     )
     mapped = total_over(mapped, ROW)
-    half = (3 * K // 4, BLOCK)
-    kept, sent = local_call(image_kernel, [half, half], place, mapped, cov_near)
-    swap = [(0, 1), (1, 0)]
-    mine = sent_to_all(kept + lax.ppermute(sent, "core", swap), "z").sum(axis=0)
-    other = lax.ppermute(mine, "core", swap)
-    mapped, grams = local_call(
-        first_factor_kernel, [(K, BLOCK), (4, K // 2, 2 * K)], place, mine, other
-    )
+    (terms,) = local_call(image_kernel, [(3 * K // 2, BLOCK)], mapped, cov_near)
+    both = lax.all_gather(terms.reshape(2, 3 * K // 4, BLOCK), "core")
+    mine = lax.dynamic_index_in_dim(both, lax.axis_index("core"), 1, keepdims=False).sum(axis=0)
+    mine = sent_to_all(mine, "z").sum(axis=0)
+    total = lax.all_gather(mine, "core", tiled=True)
+    mapped, grams = local_call(first_factor_kernel, [(K, BLOCK), (4, K // 2, 2 * K)], total)
     grams = sent_to_all(exchanged(grams, "row_0").sum(axis=0), "row_1")
     (basis,) = local_call(last_factor_kernel, [(K, BLOCK)], grams, mapped, result=jax.ShapeDtypeStruct)
     return (cov, basis)

time: 137 us -> 134 us (0.978)
  starting transfers between devices: 45 us -> 36.4 us
  waiting for transfers between devices: 7.78 us -> 14.9 us
  Pallas kernels: 11.3 us -> 9.92 us
    ppermute x2 -> x0, starting transfers between devices: 12.4 us -> none  [the longest x1 8.55 us: per_device(): mine = sent_to_all(kept + lax.ppermute(sent, 'core', swap), 'z').sum(axis=0)]
    all_to_all x3 -> x2, blocking collectives: 42.3 us -> 30.5 us  [sent_to_all(): return lax.all_to_all(copies, axis, split_axis=0, concat_axis=0, tiled=True)]
    all_gather x0 -> x2, blocking collectives: none -> 11.4 us  [the longest x1 7.99 us: per_device(): both = lax.all_gather(terms.reshape(2, 3 * K // 4, BLOCK), 'core')]
    all_to_all x1 -> x2, waiting for transfers between devices: 1.55 us -> 10.4 us  [sent_to_all(): return lax.all_to_all(copies, axis, split_axis=0, concat_axis=0, tiled=True)]
    all_to_all x1 -> x2, starting transfers between devices: 7.28 us -> 11.1 us  [sent_to_all(): return lax.all_to_all(copies, axis, split_axis=0, concat_axis=0, tiled=True)]
    ppermute x2 -> x0, waiting for transfers between devices: 1.65 us -> none  [the longest x1 0.83 us: per_device(): mine = sent_to_all(kept + lax.ppermute(sent, 'core', swap), 'z').sum(axis=0)]
  transfers between devices with their start and end apart: 7 -> 6, of which waited for: 5 -> 4; matrix products, arithmetic and copies ran while one was open for 1% -> 1% of each run, Pallas kernels for 0% -> 0%
where the time goes in v5:
time: 134 us; the launch traced here: 133 us
  blocking collectives  66.9 us (50%)
  starting transfers between devices  36.4 us (27%)
  waiting for transfers between devices  14.9 us (11%)
  Pallas kernels  9.92 us (7%)
  local copies, waits for them, and re-layouts  2.97 us (2%)
    all_to_all x2, blocking collectives, sent_to_all(): return lax.all_to_all(copies, axis, split_axis=0, concat_axis=0, tiled=True)  30.5 us
    all_to_all x2, blocking collectives, exchanged(): return lax.all_to_all(tiles, axis, split_axis=0, concat_axis=0, tiled=True)  25 us
    ppermute x1, starting transfers between devices, per_device(): piece = lax.ppermute(piece, EVERY, piece_routes())  15 us
    all_to_all x2, starting transfers between devices, sent_to_all(): return lax.all_to_all(copies, axis, split_axis=0, concat_axis=0, tiled=True)  11.1 us
    all_to_all x2, waiting for transfers between devices, sent_to_all(): return lax.all_to_all(copies, axis, split_axis=0, concat_axis=0, tiled=True)  10.4 us
    all_gather x1, blocking collectives, per_device(): both = lax.all_gather(terms.reshape(2, 3 * K // 4, BLOCK), 'core')  7.99 us
    ppermute x1, starting transfers between devices, per_device(): after = lax.ppermute(own, ROW, [(i, (i - 1) % 32) for i in range(32)])  6.55 us
    pallas_call x1, Pallas kernels, covariance_block(): pl.pallas_call(covariance_kernel, name='covariance_block', in_specs=[pl.B...  5.09 us
  transfers between devices with their start and end apart: 6, of which 4 were waited for; matrix products, arithmetic and copies ran while one was open for 1% of the time, Pallas kernels for 0%

profile of v5, /device:TPU:1, one launch (start us, length us, event | category | flops | bytes accessed | tf_op | source)
XLA Modules:
  0.0 133.2 jit_solution(7437834931498316562)
XLA Ops:
  0.6 0.0 copy-start.1
  0.7 0.8 copy-done.1
  1.5 0.0 copy-start.3
  1.5 0.6 copy-done.3
  2.1 15.0 %collective-permute-start = (bf16[32,256]{1,0:T(8,128)(2,1)S(1)}, bf16[32,256]{1,0:T(8,128)(2,1)S(1)}, u32[]{:S(2)}, u32[]{:S(2)}) collective-permute-start(bf16[32,256]{1,0:T(8,128)(2,1)S(1)} %fusion.2), channel_id=1, source_target_pairs={{0,256},{1,287},{2,303},{3,304},{4,320},{5,351},{6,367},{7,368},{8... | collective-permute-start | bytes 49160 | tf_op jit(solution)/shard_map/ppermute | solution.py:237
  17.1 0.8 collective-permute-done
  18.0 0.9 broadcast_in_dim.17
  18.8 0.0 copy-start.2
  18.8 7.3 %all-to-all-start = ((bf16[32,32,256]{2,1,0:T(8,128)(2,1)}), bf16[32,32,256]{2,1,0:T(8,128)(2,1)S(1)}, u32[]{:S(2)}, u32[]{:S(2)}) async-start(bf16[32,32,256]{2,1,0:T(8,128)(2,1)} %broadcast_in_dim.17), calls=%async_computation | async-start | bytes 1048576 | tf_op jit(solution)/shard_map/all_to_all | solution.py:40
  26.1 6.6 %collective-permute-start.1 = (bf16[128,256]{1,0:T(8,128)(2,1)S(1)}, bf16[128,256]{1,0:T(8,128)(2,1)S(1)}, u32[]{:S(2)}, u32[]{:S(2)}) collective-permute-start(bf16[128,256]{1,0:T(8,128)(2,1)S(1)} %bitcast.16), channel_id=1, source_target_pairs={{0,496},{16,0},{32,16},{48,32},{64,48},{80,64},{96,80},{112,96},{1... | collective-permute-start | bytes 196616 | tf_op jit(solution)/shard_map/ppermute | solution.py:238
  32.7 3.1 %collective-permute-start.2 = (bf16[128,256]{1,0:T(8,128)(2,1)S(1)}, bf16[128,256]{1,0:T(8,128)(2,1)S(1)}, u32[]{:S(2)}, u32[]{:S(2)}) collective-permute-start(bf16[128,256]{1,0:T(8,128)(2,1)S(1)} %bitcast.17), channel_id=1, source_target_pairs={{0,496},{16,480},{32,464},{48,448},{64,432},{80,416},{96,400},{112... | collective-permute-start | bytes 196616 | tf_op jit(solution)/shard_map/ppermute | solution.py:239
  35.8 0.7 collective-permute-start.3
  36.4 0.0 copy-done.2
  36.4 0.0 copy-start
  36.5 0.6 pad_add_fusion.place
  37.1 1.5 %all-to-all-done.pieces = bf16[32,32,256]{2,1,0:T(8,128)(2,1)S(1)} async-done(((bf16[32,32,256]{2,1,0:T(8,128)(2,1)}), bf16[32,32,256]{2,1,0:T(8,128)(2,1)S(1)}, u32[]{:S(2)}, u32[]{:S(2)}) %all-to-all-start) | async-done | bytes 524320 | tf_op jit(solution)/shard_map/all_to_all | solution.py:40
  38.6 0.6 slice_convert_fusion
  39.2 0.0 collective-permute-done.1.after
  39.2 3.7 %collective-permute-done.2.mirror = bf16[128,256]{1,0:T(8,128)(2,1)S(1)} collective-permute-done((bf16[128,256]{1,0:T(8,128)(2,1)S(1)}, bf16[128,256]{1,0:T(8,128)(2,1)S(1)}, u32[]{:S(2)}, u32[]{:S(2)}) %collective-permute-start.2) | collective-permute-done | bytes 65568 | tf_op jit(solution)/shard_map/ppermute | solution.py:239
  42.9 0.0 collective-permute-done.3.mirror_after
  42.9 0.0 copy-done
  42.9 5.1 %covariance_block.1 = (f32[128,256]{1,0:T(8,128)}, f32[128,256]{1,0:T(8,128)S(1)}, f32[32,4,128]{2,1,0:T(4,128)S(1)}) custom-call(s32[2]{0:T(128)} %pad_add_fusion.place, s32[16,3]{1,0:T(8,128)} %bitcast.24, bf16[128,256]{1,0:T(8,128)(2,1)S(1)} %bitcast.19, bf16[128,256]{1,0:T(8,128)(2,1)S(1)} %collective-permute-done.1.after, ...), custom_call_target="tpu_custom_call" | custom-call | tf_op jit(solution)/shard_map/covariance_block/pallas_call | solution.py:113
  48.0 18.1 %all_to_all.30 = f32[32,4,128]{2,1,0:T(4,128)S(1)} all-to-all(f32[32,4,128]{2,1,0:T(4,128)S(1)} %get-tuple-element.8), channel_id=1, replica_groups=mesh['row_0'=4,'row_1'=8,'z'=8,'core'=2] {'row_0','row_1'}, dimensions={0} | all-to-all | bytes 131072 | tf_op jit(solution)/shard_map/all_to_all | solution.py:206
  66.2 0.6 broadcast_in_dim.18
  66.8 3.8 %all-to-all-start.2 = ((f32[32,4,128]{2,1,0:T(4,128)}), f32[32,4,128]{2,1,0:T(4,128)S(1)}, u32[]{:S(2)}, u32[]{:S(2)}) async-start(f32[32,4,128]{2,1,0:T(4,128)} %broadcast_in_dim.18), calls=%async_computation.2 | async-start | bytes 131072 | tf_op jit(solution)/shard_map/all_to_all | solution.py:40
  70.6 8.9 %all-to-all-done.2.mapped = f32[32,4,128]{2,1,0:T(4,128)S(1)} async-done(((f32[32,4,128]{2,1,0:T(4,128)}), f32[32,4,128]{2,1,0:T(4,128)S(1)}, u32[]{:S(2)}, u32[]{:S(2)}) %all-to-all-start.2) | async-done | bytes 65568 | tf_op jit(solution)/shard_map/all_to_all | solution.py:40
  79.5 0.3 shard_map.59
  79.8 8.0 %all_gather.6 = f32[2,2,48,128]{3,2,1,0:T(8,128)S(1)} all-gather(f32[1,2,48,128]{3,2,1,0:T(8,128)S(1)} %bitcast.21), channel_id=1, replica_groups=mesh['row_0'=4,'row_1'=8,'z'=8,'core'=2] {'core'}, dimensions={0}, use_global_device_ids=true | all-gather | bytes 147456 | tf_op jit(solution)/shard_map/all_gather | solution.py:249
  87.9 20.1 %all_to_all.31 = f32[8,48,128]{2,1,0:T(8,128)S(1)} all-to-all(f32[8,48,128]{2,1,0:T(8,128)S(1)} %broadcast_in_dim.19), channel_id=1, replica_groups=mesh['row_0'=4,'row_1'=8,'z'=8,'core'=2] {'z'}, dimensions={0} | all-to-all | bytes 393216 | tf_op jit(solution)/shard_map/all_to_all | solution.py:40
  108.0 3.5 %all_gather.7.total = f32[96,128]{1,0:T(8,128)S(1)} all-gather(f32[48,128]{1,0:T(8,128)S(1)} %reduce_sum.38), channel_id=1, replica_groups=mesh['row_0'=4,'row_1'=8,'z'=8,'core'=2] {'core'}, dimensions={0}, use_global_device_ids=true | all-gather | bytes 73728 | tf_op jit(solution)/shard_map/all_gather | solution.py:252
  111.5 2.1 %shard_map.60 = (f32[64,128]{1,0:T(8,128)S(1)}, f32[4,32,128]{2,1,0:T(8,128)S(1)}) custom-call(f32[96,128]{1,0:T(8,128)S(1)} %all_gather.7.total), custom_call_target="tpu_custom_call" | custom-call | tf_op jit(solution)/shard_map/pallas_call | solution.py:198
  113.5 6.9 %all_to_all.32 = f32[4,32,128]{2,1,0:T(8,128)S(1)} all-to-all(f32[4,32,128]{2,1,0:T(8,128)S(1)} %get-tuple-element.10), channel_id=1, replica_groups=mesh['row_0'=4,'row_1'=8,'z'=8,'core'=2] {'row_0'}, dimensions={0} | all-to-all | bytes 131072 | tf_op jit(solution)/shard_map/all_to_all | solution.py:206
  120.4 10.3 %all_to_all.33.grams = f32[8,32,128]{2,1,0:T(8,128)S(1)} all-to-all(f32[8,32,128]{2,1,0:T(8,128)S(1)} %broadcast_in_dim.20), channel_id=1, replica_groups=mesh['row_0'=4,'row_1'=8,'z'=8,'core'=2] {'row_1'}, dimensions={0} | all-to-all | bytes 262144 | tf_op jit(solution)/shard_map/all_to_all | solution.py:40
  130.8 2.4 %shard_map.61 = f32[64,128]{1,0:T(8,128)} custom-call(f32[8,32,128]{2,1,0:T(8,128)S(1)} %all_to_all.33.grams, f32[64,128]{1,0:T(8,128)S(1)} %get-tuple-element.11.mapped), custom_call_target="tpu_custom_call" | custom-call | tf_op jit(solution)/shard_map/pallas_call | solution.py:198
  (11 shorter events, 0.1 us)
Async XLA Ops:
  0.6 0.8 copy-start.1
  1.5 0.7 copy-start.3
  2.1 15.8 %collective-permute-start = (bf16[32,256]{1,0:T(8,128)(2,1)S(1)}, bf16[32,256]{1,0:T(8,128)(2,1)S(1)}, u32[]{:S(2)}, u32[]{:S(2)}) collective-permute-start(bf16[32,256]{1,0:T(8,128)(2,1)S(1)} %fusion.2), channel_id=1, source_target_pairs={{0,256},{1,287},{2,303},{3,304},{4,320},{5,351},{6,367},{7,368},{8... | collective-permute-start | bytes 49160 | tf_op jit(solution)/shard_map/ppermute | solution.py:237
  18.8 17.6 %copy-start.2 = (bf16[128,2,128]{2,1,0:T(2,128)(2,1)S(1)}, bf16[128,2,128]{2,1,0:T(2,128)(2,1)}, u32[]{:S(2)}) copy-start(bf16[128,2,128]{2,1,0:T(2,128)(2,1)} %param.5) | copy-start | bytes 196612
  18.8 19.8 %all-to-all-start = ((bf16[32,32,256]{2,1,0:T(8,128)(2,1)}), bf16[32,32,256]{2,1,0:T(8,128)(2,1)S(1)}, u32[]{:S(2)}, u32[]{:S(2)}) async-start(bf16[32,32,256]{2,1,0:T(8,128)(2,1)} %broadcast_in_dim.17), calls=%async_computation | async-start | bytes 1048576 | tf_op jit(solution)/shard_map/all_to_all | solution.py:40
  26.1 13.1 %collective-permute-start.1 = (bf16[128,256]{1,0:T(8,128)(2,1)S(1)}, bf16[128,256]{1,0:T(8,128)(2,1)S(1)}, u32[]{:S(2)}, u32[]{:S(2)}) collective-permute-start(bf16[128,256]{1,0:T(8,128)(2,1)S(1)} %bitcast.16), channel_id=1, source_target_pairs={{0,496},{16,0},{32,16},{48,32},{64,48},{80,64},{96,80},{112,96},{1... | collective-permute-start | bytes 196616 | tf_op jit(solution)/shard_map/ppermute | solution.py:238
  32.7 10.3 %collective-permute-start.2 = (bf16[128,256]{1,0:T(8,128)(2,1)S(1)}, bf16[128,256]{1,0:T(8,128)(2,1)S(1)}, u32[]{:S(2)}, u32[]{:S(2)}) collective-permute-start(bf16[128,256]{1,0:T(8,128)(2,1)S(1)} %bitcast.17), channel_id=1, source_target_pairs={{0,496},{16,480},{32,464},{48,448},{64,432},{80,416},{96,400},{112... | collective-permute-start | bytes 196616 | tf_op jit(solution)/shard_map/ppermute | solution.py:239
  35.8 7.2 %collective-permute-start.3 = (bf16[128,256]{1,0:T(8,128)(2,1)S(1)}, bf16[128,256]{1,0:T(8,128)(2,1)S(1)}, u32[]{:S(2)}, u32[]{:S(2)}) collective-permute-start(bf16[128,256]{1,0:T(8,128)(2,1)S(1)} %bitcast.18), channel_id=1, source_target_pairs={{0,0},{16,496},{32,480},{48,464},{64,448},{80,432},{96,416},{112,4... | collective-permute-start | bytes 196616 | tf_op jit(solution)/shard_map/ppermute | solution.py:240
  36.4 6.5 %copy-start = (f32[64,128]{1,0:T(8,128)S(1)}, f32[64,128]{1,0:T(8,128)}, u32[]{:S(2)}) copy-start(f32[64,128]{1,0:T(8,128)} %basis.1) | copy-start | bytes 98308
  66.8 12.7 %all-to-all-start.2 = ((f32[32,4,128]{2,1,0:T(4,128)}), f32[32,4,128]{2,1,0:T(4,128)S(1)}, u32[]{:S(2)}, u32[]{:S(2)}) async-start(f32[32,4,128]{2,1,0:T(4,128)} %broadcast_in_dim.18), calls=%async_computation.2 | async-start | bytes 131072 | tf_op jit(solution)/shard_map/all_to_all | solution.py:40

commit v6 on v5

--- a/solution.py
+++ b/solution.py
@@ -41,11 +41,15 @@
 
 
 def covariance_kernel(
-    place, offsets, own, after, mirror, mirror_after, tail, pieces, basis,
+    own, after, mirror, mirror_after, tail, pieces, basis,
     cov, cov_near, mapped, row_w, row_z, col_w, col_z, acc,
 ):
-    r = place[0]
-    c = place[1]
+    r = lax.axis_index(ROW)
+    c = lax.axis_index(SHIFT)
+    offsets = []
+    for q in range(16):
+        held = pieces[q, 16:, :SNAPS].astype(jnp.float32).astype(jnp.int32)
+        offsets += [held[i, 0] for i in range(3)]
     flip = (
         lax.broadcasted_iota(jnp.int32, (BLOCK, BLOCK), 0)
         + lax.broadcasted_iota(jnp.int32, (BLOCK, BLOCK), 1)
@@ -83,10 +87,10 @@
 
     acc[...] = jnp.zeros(acc.shape, jnp.float32)
 
-    def step(at, carry):
+    def step(carry):
         left, right = [], []
         for u in range(3 * GROUP):
-            o = offsets[at * GROUP + u // 3, u % 3]
+            o = offsets[u]
             for plane in range(2):
                 left.append(
                     (row_w[plane, pl.ds(o, BLOCK), :] + row_z[plane, pl.ds(BLOCK - o, BLOCK), :])
@@ -99,7 +103,7 @@
         acc[...] += dot_nt(jnp.concatenate(left, axis=1), jnp.concatenate(right, axis=1))
         return carry
 
-    step(0, 0)
+    step(0)
     block = acc[...] * (1.0 / (SNAPS * SHIFTS))
     cov[...] = block
     cov_near[...] = block
@@ -108,12 +112,12 @@
         mapped[p] = image[4 * (p // 2) : 4 * (p // 2) + 4, SNAPS * (p % 2) : SNAPS * (p % 2) + SNAPS]
 
 
-def covariance_block(place, offsets, own, after, mirror, mirror_after, tail, pieces, basis):
+def covariance_block(own, after, mirror, mirror_after, tail, pieces, basis):
     vmem = pl.BlockSpec(memory_space=pltpu.VMEM)
     return pl.pallas_call(
         covariance_kernel,
         name="covariance_block",
-        in_specs=[pl.BlockSpec(memory_space=pltpu.SMEM)] * 2 + [vmem] * 7,
+        in_specs=[vmem] * 7,
         out_specs=[vmem] * 3,
         out_shape=[
             jax.ShapeDtypeStruct((BLOCK, 2 * BLOCK), jnp.float32),
@@ -127,7 +131,7 @@
             pltpu.VMEM((2, 3 * BLOCK, SNAPS), jnp.float32),
             pltpu.VMEM((BLOCK, 2 * BLOCK), jnp.float32),
         ],
-    )(place, offsets, *[near(x) for x in (own, after, mirror, mirror_after, tail, pieces, basis)])
+    )(*[near(x) for x in (own, after, mirror, mirror_after, tail, pieces, basis)])
 
 
 def inverse_factor(gram):
@@ -227,10 +231,12 @@
 def per_device(snapshots, tail_sensors, shift_offsets, start_basis):
     r = lax.axis_index(ROW)
     c = lax.axis_index(SHIFT)
-    own = snapshots.reshape(BLOCK, 2 * SNAPS)
     tail = tail_sensors.reshape(BLOCK, 2 * SNAPS)
     offsets = jnp.zeros((16, 2 * SNAPS), jnp.bfloat16)
-    offsets = lax.dynamic_update_slice(offsets, shift_offsets.astype(jnp.bfloat16)[None], (0, 0))
+    offsets = lax.dynamic_update_slice(offsets, shift_offsets.astype(jnp.bfloat16)[:, None], (0, 0))
+    core = lax.axis_index("core").astype(jnp.uint32)
+    own, core, offsets = lax.optimization_barrier((snapshots, core, offsets))
+    own = own.reshape(BLOCK, 2 * SNAPS)
     odd_piece = jnp.concatenate([lax.dynamic_slice_in_dim(own, 16 * (c // 2), 16, 0), offsets], 0)
     even_piece = lax.dynamic_slice_in_dim(own, 32 * (c // 4), 32, 0)
     piece = jnp.where(r % 2 == 1, odd_piece, even_piece)
@@ -239,15 +245,13 @@
     mirror = lax.ppermute(own, ROW, [(i, 31 - i) for i in range(32)])
     mirror_after = lax.ppermute(own, ROW, [(i, (32 - i) % 32) for i in range(32)])
     pieces = sent_to_all(piece, ROW)
-    every_offset = pieces[:16, 16, :3].astype(jnp.int32)
-    place = jnp.stack([r, c]).astype(jnp.int32)
     cov, cov_near, mapped = covariance_block(
-        place, every_offset, own, after, mirror, mirror_after, tail, pieces, start_basis
+        own, after, mirror, mirror_after, tail, pieces, start_basis
     )
     mapped = total_over(mapped, ROW)
     (terms,) = local_call(image_kernel, [(3 * K // 2, BLOCK)], mapped, cov_near)
     both = lax.all_gather(terms.reshape(2, 3 * K // 4, BLOCK), "core")
-    mine = lax.dynamic_index_in_dim(both, lax.axis_index("core"), 1, keepdims=False).sum(axis=0)
+    mine = lax.dynamic_index_in_dim(both, core, 1, keepdims=False).sum(axis=0)
     mine = sent_to_all(mine, "z").sum(axis=0)
     total = lax.all_gather(mine, "core", tiled=True)
     mapped, grams = local_call(first_factor_kernel, [(K, BLOCK), (4, K // 2, 2 * K)], total)

time: 134 us -> 131 us (0.978)
  blocking collectives: 66.9 us -> 78.9 us
  waiting for transfers between devices: 14.9 us -> 7.32 us
  starting transfers between devices: 36.4 us -> 32.5 us
    all_to_all x2 -> x3, blocking collectives: 30.5 us -> 42.3 us  [sent_to_all(): return lax.all_to_all(copies, axis, split_axis=0, concat_axis=0, tiled=True)]
    all_to_all x2 -> x1, waiting for transfers between devices: 10.4 us -> 0.01 us  [sent_to_all(): return lax.all_to_all(copies, axis, split_axis=0, concat_axis=0, tiled=True)]
    all_to_all x2 -> x1, starting transfers between devices: 11.1 us -> 7.28 us  [sent_to_all(): return lax.all_to_all(copies, axis, split_axis=0, concat_axis=0, tiled=True)]
    ppermute x1, waiting for transfers between devices: 0.01 us -> 1.78 us  [per_device(): after = lax.ppermute(own, ROW, [(i, (i - 1) % 32) for i in range(32)])]
  transfers between devices with their start and end apart: 6 -> 5, of which waited for: 4 -> 3; matrix products, arithmetic and copies ran while one was open for 1% -> 0% of each run, Pallas kernels for 0% -> 0%
where the time goes in v6:
time: 131 us; the launch traced here: 130 us
  blocking collectives  78.9 us (60%)
  starting transfers between devices  32.5 us (25%)
  Pallas kernels  9.13 us (7%)
  waiting for transfers between devices  7.32 us (6%)
  local copies, waits for them, and re-layouts  1.71 us (1%)
    all_to_all x3, blocking collectives, sent_to_all(): return lax.all_to_all(copies, axis, split_axis=0, concat_axis=0, tiled=True)  42.3 us
    all_to_all x2, blocking collectives, exchanged(): return lax.all_to_all(tiles, axis, split_axis=0, concat_axis=0, tiled=True)  25 us
    ppermute x1, starting transfers between devices, per_device(): piece = lax.ppermute(piece, EVERY, piece_routes())  15 us
    all_gather x1, blocking collectives, per_device(): both = lax.all_gather(terms.reshape(2, 3 * K // 4, BLOCK), 'core')  8.16 us
    all_to_all x1, starting transfers between devices, sent_to_all(): return lax.all_to_all(copies, axis, split_axis=0, concat_axis=0, tiled=True)  7.28 us
    ppermute x1, starting transfers between devices, per_device(): after = lax.ppermute(own, ROW, [(i, (i - 1) % 32) for i in range(32)])  6.55 us
    pallas_call x3, Pallas kernels, local_call(): pl.pallas_call(kernel, in_specs=[pl.BlockSpec(memory_space=space) for spa...  4.83 us
    ppermute x1, waiting for transfers between devices, per_device(): mirror = lax.ppermute(own, ROW, [(i, 31 - i) for i in range(32)])  4.69 us
  transfers between devices with their start and end apart: 5, of which 3 were waited for; matrix products, arithmetic and copies ran while one was open for 0% of the time, Pallas kernels for 0%

profile of v6, /device:TPU:1, one launch (start us, length us, event | category | flops | bytes accessed | tf_op | source)
XLA Modules:
  0.0 130.5 jit_solution(3648235251960401822)
XLA Ops:
  0.6 0.0 copy-start.1
  0.7 0.0 copy-start.3
  0.7 0.6 copy-done.3
  1.3 0.1 copy.8
  1.5 0.0 copy-done.1
  1.5 15.0 %collective-permute-start.3 = (bf16[32,256]{1,0:T(8,128)(2,1)S(1)}, bf16[32,256]{1,0:T(8,128)(2,1)S(1)}, u32[]{:S(2)}, u32[]{:S(2)}) collective-permute-start(bf16[32,256]{1,0:T(8,128)(2,1)S(1)} %maximum_select_fusion), channel_id=1, source_target_pairs={{0,256},{1,287},{2,303},{3,304},{4,320},{5,351},{6,367},{7,368},{8... | collective-permute-start | bytes 49160 | tf_op jit(solution)/shard_map/ppermute | solution.py:243
  16.5 0.8 collective-permute-done.3
  17.4 0.8 broadcast_in_dim.17
  18.2 0.0 copy-start.2
  18.2 7.3 %all-to-all-start = ((bf16[32,32,256]{2,1,0:T(8,128)(2,1)}), bf16[32,32,256]{2,1,0:T(8,128)(2,1)S(1)}, u32[]{:S(2)}, u32[]{:S(2)}) async-start(bf16[32,32,256]{2,1,0:T(8,128)(2,1)} %broadcast_in_dim.17), calls=%async_computation | async-start | bytes 1048576 | tf_op jit(solution)/shard_map/all_to_all | solution.py:40
  25.5 6.6 %collective-permute-start = (bf16[128,256]{1,0:T(8,128)(2,1)S(1)}, bf16[128,256]{1,0:T(8,128)(2,1)S(1)}, u32[]{:S(2)}, u32[]{:S(2)}) collective-permute-start(bf16[128,256]{1,0:T(8,128)(2,1)S(1)} %bitcast.13), channel_id=1, source_target_pairs={{0,496},{16,0},{32,16},{48,32},{64,48},{80,64},{96,80},{112,96},{1... | collective-permute-start | bytes 196616 | tf_op jit(solution)/shard_map/ppermute | solution.py:244
  32.0 3.1 %collective-permute-start.1 = (bf16[128,256]{1,0:T(8,128)(2,1)S(1)}, bf16[128,256]{1,0:T(8,128)(2,1)S(1)}, u32[]{:S(2)}, u32[]{:S(2)}) collective-permute-start(bf16[128,256]{1,0:T(8,128)(2,1)S(1)} %bitcast.14), channel_id=1, source_target_pairs={{0,496},{16,480},{32,464},{48,448},{64,432},{80,416},{96,400},{112... | collective-permute-start | bytes 196616 | tf_op jit(solution)/shard_map/ppermute | solution.py:245
  35.1 0.7 collective-permute-start.2
  35.8 0.0 copy-done.2
  35.8 0.0 copy-start
  35.9 1.8 %collective-permute-done.after = bf16[128,256]{1,0:T(8,128)(2,1)S(1)} collective-permute-done((bf16[128,256]{1,0:T(8,128)(2,1)S(1)}, bf16[128,256]{1,0:T(8,128)(2,1)S(1)}, u32[]{:S(2)}, u32[]{:S(2)}) %collective-permute-start) | collective-permute-done | bytes 65568 | tf_op jit(solution)/shard_map/ppermute | solution.py:244
  37.6 4.7 %collective-permute-done.1.mirror = bf16[128,256]{1,0:T(8,128)(2,1)S(1)} collective-permute-done((bf16[128,256]{1,0:T(8,128)(2,1)S(1)}, bf16[128,256]{1,0:T(8,128)(2,1)S(1)}, u32[]{:S(2)}, u32[]{:S(2)}) %collective-permute-start.1) | collective-permute-done | bytes 65568 | tf_op jit(solution)/shard_map/ppermute | solution.py:245
  42.3 0.0 collective-permute-done.2.mirror_after
  42.3 0.0 all-to-all-done.pieces
  42.3 0.0 copy-done
  42.3 4.3 %covariance_block.1 = (f32[128,256]{1,0:T(8,128)}, f32[128,256]{1,0:T(8,128)S(1)}, f32[32,4,128]{2,1,0:T(4,128)S(1)}) custom-call(bf16[128,256]{1,0:T(8,128)(2,1)S(1)} %bitcast.16, bf16[128,256]{1,0:T(8,128)(2,1)S(1)} %collective-permute-done.after, bf16[128,256]{1,0:T(8,128)(2,1)S(1)} %collective-permute-done.1.mirror, ...), custom_call_target="tpu_custom_call" | custom-call | tf_op jit(solution)/shard_map/covariance_block/pallas_call | solution.py:117
  46.6 18.1 %all_to_all.30 = f32[32,4,128]{2,1,0:T(4,128)S(1)} all-to-all(f32[32,4,128]{2,1,0:T(4,128)S(1)} %get-tuple-element.13), channel_id=1, replica_groups=mesh['row_0'=4,'row_1'=8,'z'=8,'core'=2] {'row_0','row_1'}, dimensions={0} | all-to-all | bytes 131072 | tf_op jit(solution)/shard_map/all_to_all | solution.py:210
  64.8 11.8 %all_to_all.31.mapped = f32[32,4,128]{2,1,0:T(4,128)S(1)} all-to-all(f32[32,4,128]{2,1,0:T(4,128)S(1)} %broadcast_in_dim.18), channel_id=1, replica_groups=mesh['row_0'=4,'row_1'=8,'z'=8,'core'=2] {'row_0','row_1'}, dimensions={0} | all-to-all | bytes 131072 | tf_op jit(solution)/shard_map/all_to_all | solution.py:40
  76.6 0.3 shard_map.59
  77.0 8.2 %all_gather.6 = f32[2,2,48,128]{3,2,1,0:T(8,128)S(1)} all-gather(f32[1,2,48,128]{3,2,1,0:T(8,128)S(1)} %bitcast.18), channel_id=1, replica_groups=mesh['row_0'=4,'row_1'=8,'z'=8,'core'=2] {'core'}, dimensions={0}, use_global_device_ids=true | all-gather | bytes 147456 | tf_op jit(solution)/shard_map/all_gather | solution.py:253
  85.1 20.1 %all_to_all.32 = f32[8,48,128]{2,1,0:T(8,128)S(1)} all-to-all(f32[8,48,128]{2,1,0:T(8,128)S(1)} %broadcast_in_dim.19), channel_id=1, replica_groups=mesh['row_0'=4,'row_1'=8,'z'=8,'core'=2] {'z'}, dimensions={0} | all-to-all | bytes 393216 | tf_op jit(solution)/shard_map/all_to_all | solution.py:40
  105.3 3.5 %all_gather.7.total = f32[96,128]{1,0:T(8,128)S(1)} all-gather(f32[48,128]{1,0:T(8,128)S(1)} %reduce_sum.38), channel_id=1, replica_groups=mesh['row_0'=4,'row_1'=8,'z'=8,'core'=2] {'core'}, dimensions={0}, use_global_device_ids=true | all-gather | bytes 73728 | tf_op jit(solution)/shard_map/all_gather | solution.py:256
  108.8 2.1 %shard_map.60 = (f32[64,128]{1,0:T(8,128)S(1)}, f32[4,32,128]{2,1,0:T(8,128)S(1)}) custom-call(f32[96,128]{1,0:T(8,128)S(1)} %all_gather.7.total), custom_call_target="tpu_custom_call" | custom-call | tf_op jit(solution)/shard_map/pallas_call | solution.py:202
  110.8 6.9 %all_to_all.33 = f32[4,32,128]{2,1,0:T(8,128)S(1)} all-to-all(f32[4,32,128]{2,1,0:T(8,128)S(1)} %get-tuple-element.16), channel_id=1, replica_groups=mesh['row_0'=4,'row_1'=8,'z'=8,'core'=2] {'row_0'}, dimensions={0} | all-to-all | bytes 131072 | tf_op jit(solution)/shard_map/all_to_all | solution.py:210
  117.7 10.3 %all_to_all.34.grams = f32[8,32,128]{2,1,0:T(8,128)S(1)} all-to-all(f32[8,32,128]{2,1,0:T(8,128)S(1)} %broadcast_in_dim.20), channel_id=1, replica_groups=mesh['row_0'=4,'row_1'=8,'z'=8,'core'=2] {'row_1'}, dimensions={0} | all-to-all | bytes 262144 | tf_op jit(solution)/shard_map/all_to_all | solution.py:40
  128.1 2.4 %shard_map.61 = f32[64,128]{1,0:T(8,128)} custom-call(f32[8,32,128]{2,1,0:T(8,128)S(1)} %all_to_all.34.grams, f32[64,128]{1,0:T(8,128)S(1)} %get-tuple-element.17.mapped), custom_call_target="tpu_custom_call" | custom-call | tf_op jit(solution)/shard_map/pallas_call | solution.py:202
  (13 shorter events, 0.2 us)
Async XLA Ops:
  0.6 0.8 copy-start.1
  0.7 0.7 copy-start.3
  1.5 15.8 %collective-permute-start.3 = (bf16[32,256]{1,0:T(8,128)(2,1)S(1)}, bf16[32,256]{1,0:T(8,128)(2,1)S(1)}, u32[]{:S(2)}, u32[]{:S(2)}) collective-permute-start(bf16[32,256]{1,0:T(8,128)(2,1)S(1)} %maximum_select_fusion), channel_id=1, source_target_pairs={{0,256},{1,287},{2,303},{3,304},{4,320},{5,351},{6,367},{7,368},{8... | collective-permute-start | bytes 49160 | tf_op jit(solution)/shard_map/ppermute | solution.py:243
  18.2 17.6 %copy-start.2 = (bf16[128,2,128]{2,1,0:T(2,128)(2,1)S(1)}, bf16[128,2,128]{2,1,0:T(2,128)(2,1)}, u32[]{:S(2)}) copy-start(bf16[128,2,128]{2,1,0:T(2,128)(2,1)} %param.5) | copy-start | bytes 196612
  18.2 24.1 %all-to-all-start = ((bf16[32,32,256]{2,1,0:T(8,128)(2,1)}), bf16[32,32,256]{2,1,0:T(8,128)(2,1)S(1)}, u32[]{:S(2)}, u32[]{:S(2)}) async-start(bf16[32,32,256]{2,1,0:T(8,128)(2,1)} %broadcast_in_dim.17), calls=%async_computation | async-start | bytes 1048576 | tf_op jit(solution)/shard_map/all_to_all | solution.py:40
  25.5 12.1 %collective-permute-start = (bf16[128,256]{1,0:T(8,128)(2,1)S(1)}, bf16[128,256]{1,0:T(8,128)(2,1)S(1)}, u32[]{:S(2)}, u32[]{:S(2)}) collective-permute-start(bf16[128,256]{1,0:T(8,128)(2,1)S(1)} %bitcast.13), channel_id=1, source_target_pairs={{0,496},{16,0},{32,16},{48,32},{64,48},{80,64},{96,80},{112,96},{1... | collective-permute-start | bytes 196616 | tf_op jit(solution)/shard_map/ppermute | solution.py:244
  32.0 10.3 %collective-permute-start.1 = (bf16[128,256]{1,0:T(8,128)(2,1)S(1)}, bf16[128,256]{1,0:T(8,128)(2,1)S(1)}, u32[]{:S(2)}, u32[]{:S(2)}) collective-permute-start(bf16[128,256]{1,0:T(8,128)(2,1)S(1)} %bitcast.14), channel_id=1, source_target_pairs={{0,496},{16,480},{32,464},{48,448},{64,432},{80,416},{96,400},{112... | collective-permute-start | bytes 196616 | tf_op jit(solution)/shard_map/ppermute | solution.py:245
  35.1 7.2 %collective-permute-start.2 = (bf16[128,256]{1,0:T(8,128)(2,1)S(1)}, bf16[128,256]{1,0:T(8,128)(2,1)S(1)}, u32[]{:S(2)}, u32[]{:S(2)}) collective-permute-start(bf16[128,256]{1,0:T(8,128)(2,1)S(1)} %bitcast.15), channel_id=1, source_target_pairs={{0,0},{16,496},{32,480},{48,464},{64,448},{80,432},{96,416},{112,4... | collective-permute-start | bytes 196616 | tf_op jit(solution)/shard_map/ppermute | solution.py:246
  35.8 6.5 %copy-start = (f32[64,128]{1,0:T(8,128)S(1)}, f32[64,128]{1,0:T(8,128)}, u32[]{:S(2)}) copy-start(f32[64,128]{1,0:T(8,128)} %basis.1) | copy-start | bytes 98308

commit v7 on v6

--- a/solution.py
+++ b/solution.py
@@ -38,6 +38,17 @@
 def sent_to_all(x, axis):
     copies = jnp.broadcast_to(x, (lax.axis_size(axis), *x.shape))
     return lax.all_to_all(copies, axis, split_axis=0, concat_axis=0, tiled=True)
+
+
+def copies_kernel(piece, copies):
+    for i in range(copies.shape[0]):
+        copies[i] = piece[...]
+
+
+def copies_of(piece, count):
+    return pl.pallas_call(
+        copies_kernel, name="copies", out_shape=pltpu.VMEM((count, *piece.shape), piece.dtype)
+    )(near(piece))
 
 
 def covariance_kernel(
@@ -244,7 +255,7 @@
     after = lax.ppermute(own, ROW, [(i, (i - 1) % 32) for i in range(32)])
     mirror = lax.ppermute(own, ROW, [(i, 31 - i) for i in range(32)])
     mirror_after = lax.ppermute(own, ROW, [(i, (32 - i) % 32) for i in range(32)])
-    pieces = sent_to_all(piece, ROW)
+    pieces = exchanged(copies_of(piece, lax.axis_size(ROW)), ROW)
     cov, cov_near, mapped = covariance_block(
         own, after, mirror, mirror_after, tail, pieces, start_basis
     )
@@ -254,8 +265,8 @@
     mine = lax.dynamic_index_in_dim(both, core, 1, keepdims=False).sum(axis=0)
     mine = sent_to_all(mine, "z").sum(axis=0)
     total = lax.all_gather(mine, "core", tiled=True)
-    mapped, grams = local_call(first_factor_kernel, [(K, BLOCK), (4, K // 2, 2 * K)], total)
-    grams = sent_to_all(exchanged(grams, "row_0").sum(axis=0), "row_1")
+    mapped, grams = local_call(first_factor_kernel, [(K, BLOCK), (8, K // 2, 2 * K)], total)
+    grams = sent_to_all(exchanged(grams, "row_1").sum(axis=0), "row_0")
     (basis,) = local_call(last_factor_kernel, [(K, BLOCK)], grams, mapped, result=jax.ShapeDtypeStruct)
     return (cov, basis)
 

time: 131 us -> 132 us (level)
    all_to_all x2, blocking collectives: 25 us -> 28.9 us  [exchanged(): return lax.all_to_all(tiles, axis, split_axis=0, concat_axis=0, tiled=True)]
    all_to_all x3, blocking collectives: 42.3 us -> 38.8 us  [sent_to_all(): return lax.all_to_all(copies, axis, split_axis=0, concat_axis=0, tiled=True)]
where the time goes in v7:
time: 132 us; the launch traced here: 131 us
  blocking collectives  79.3 us (60%)
  starting transfers between devices  32.5 us (25%)
  Pallas kernels  9.96 us (8%)
  waiting for transfers between devices  7.32 us (6%)
    all_to_all x3, blocking collectives, sent_to_all(): return lax.all_to_all(copies, axis, split_axis=0, concat_axis=0, tiled=True)  38.8 us
    all_to_all x2, blocking collectives, exchanged(): return lax.all_to_all(tiles, axis, split_axis=0, concat_axis=0, tiled=True)  28.9 us
    ppermute x1, starting transfers between devices, per_device(): piece = lax.ppermute(piece, EVERY, piece_routes())  15 us
    all_gather x1, blocking collectives, per_device(): both = lax.all_gather(terms.reshape(2, 3 * K // 4, BLOCK), 'core')  8.16 us
    all_to_all x1, starting transfers between devices, exchanged(): return lax.all_to_all(tiles, axis, split_axis=0, concat_axis=0, tiled=True)  7.28 us
    ppermute x1, starting transfers between devices, per_device(): after = lax.ppermute(own, ROW, [(i, (i - 1) % 32) for i in range(32)])  6.55 us
    pallas_call x3, Pallas kernels, local_call(): pl.pallas_call(kernel, in_specs=[pl.BlockSpec(memory_space=space) for spa...  4.83 us
    ppermute x1, waiting for transfers between devices, per_device(): mirror = lax.ppermute(own, ROW, [(i, 31 - i) for i in range(32)])  4.69 us
  transfers between devices with their start and end apart: 5, of which 3 were waited for; matrix products, arithmetic and copies ran while one was open for 0% of the time, Pallas kernels for 0%

profile of v7, /device:TPU:1, one launch (start us, length us, event | category | flops | bytes accessed | tf_op | source)
XLA Modules:
  0.0 130.9 jit_solution(14515320153448356030)
XLA Ops:
  0.6 0.0 copy-start.1
  0.7 0.0 copy-start.3
  0.7 0.6 copy-done.3
  1.3 0.1 copy.8
  1.5 0.0 copy-done.1
  1.5 15.0 %collective-permute-start.3 = (bf16[32,256]{1,0:T(8,128)(2,1)S(1)}, bf16[32,256]{1,0:T(8,128)(2,1)S(1)}, u32[]{:S(2)}, u32[]{:S(2)}) collective-permute-start(bf16[32,256]{1,0:T(8,128)(2,1)S(1)} %maximum_select_fusion), channel_id=1, source_target_pairs={{0,256},{1,287},{2,303},{3,304},{4,320},{5,351},{6,367},{7,368},{8... | collective-permute-start | bytes 49160 | tf_op jit(solution)/shard_map/ppermute | solution.py:254
  16.5 0.8 collective-permute-done.3.piece
  17.4 0.8 copies.1
  18.2 0.0 copy-start.2
  18.2 7.3 %all-to-all-start = ((bf16[32,32,256]{2,1,0:T(8,128)(2,1)}), bf16[32,32,256]{2,1,0:T(8,128)(2,1)S(1)}, u32[]{:S(2)}, u32[]{:S(2)}) async-start(bf16[32,32,256]{2,1,0:T(8,128)(2,1)} %copies.1), calls=%async_computation | async-start | bytes 1048576 | tf_op jit(solution)/shard_map/all_to_all | solution.py:221
  25.5 6.6 %collective-permute-start = (bf16[128,256]{1,0:T(8,128)(2,1)S(1)}, bf16[128,256]{1,0:T(8,128)(2,1)S(1)}, u32[]{:S(2)}, u32[]{:S(2)}) collective-permute-start(bf16[128,256]{1,0:T(8,128)(2,1)S(1)} %bitcast.13), channel_id=1, source_target_pairs={{0,496},{16,0},{32,16},{48,32},{64,48},{80,64},{96,80},{112,96},{1... | collective-permute-start | bytes 196616 | tf_op jit(solution)/shard_map/ppermute | solution.py:255
  32.0 3.1 %collective-permute-start.1 = (bf16[128,256]{1,0:T(8,128)(2,1)S(1)}, bf16[128,256]{1,0:T(8,128)(2,1)S(1)}, u32[]{:S(2)}, u32[]{:S(2)}) collective-permute-start(bf16[128,256]{1,0:T(8,128)(2,1)S(1)} %bitcast.14), channel_id=1, source_target_pairs={{0,496},{16,480},{32,464},{48,448},{64,432},{80,416},{96,400},{112... | collective-permute-start | bytes 196616 | tf_op jit(solution)/shard_map/ppermute | solution.py:256
  35.1 0.7 collective-permute-start.2
  35.8 0.0 copy-done.2
  35.8 0.0 copy-start
  35.8 1.8 %collective-permute-done.after = bf16[128,256]{1,0:T(8,128)(2,1)S(1)} collective-permute-done((bf16[128,256]{1,0:T(8,128)(2,1)S(1)}, bf16[128,256]{1,0:T(8,128)(2,1)S(1)}, u32[]{:S(2)}, u32[]{:S(2)}) %collective-permute-start) | collective-permute-done | bytes 65568 | tf_op jit(solution)/shard_map/ppermute | solution.py:255
  37.6 4.7 %collective-permute-done.1.mirror = bf16[128,256]{1,0:T(8,128)(2,1)S(1)} collective-permute-done((bf16[128,256]{1,0:T(8,128)(2,1)S(1)}, bf16[128,256]{1,0:T(8,128)(2,1)S(1)}, u32[]{:S(2)}, u32[]{:S(2)}) %collective-permute-start.1) | collective-permute-done | bytes 65568 | tf_op jit(solution)/shard_map/ppermute | solution.py:256
  42.3 0.0 collective-permute-done.2.mirror_after
  42.3 0.0 all-to-all-done.pieces
  42.3 0.0 copy-done
  42.3 4.3 %covariance_block.1 = (f32[128,256]{1,0:T(8,128)}, f32[128,256]{1,0:T(8,128)S(1)}, f32[32,4,128]{2,1,0:T(4,128)S(1)}) custom-call(bf16[128,256]{1,0:T(8,128)(2,1)S(1)} %bitcast.16, bf16[128,256]{1,0:T(8,128)(2,1)S(1)} %collective-permute-done.after, bf16[128,256]{1,0:T(8,128)(2,1)S(1)} %collective-permute-done.1.mirror, ...), custom_call_target="tpu_custom_call" | custom-call | tf_op jit(solution)/shard_map/covariance_block/pallas_call | solution.py:128
  46.6 18.1 %all_to_all.30 = f32[32,4,128]{2,1,0:T(4,128)S(1)} all-to-all(f32[32,4,128]{2,1,0:T(4,128)S(1)} %get-tuple-element.13), channel_id=1, replica_groups=mesh['row_0'=4,'row_1'=8,'z'=8,'core'=2] {'row_0','row_1'}, dimensions={0} | all-to-all | bytes 131072 | tf_op jit(solution)/shard_map/all_to_all | solution.py:221
  64.8 11.8 %all_to_all.31.mapped = f32[32,4,128]{2,1,0:T(4,128)S(1)} all-to-all(f32[32,4,128]{2,1,0:T(4,128)S(1)} %broadcast_in_dim.14), channel_id=1, replica_groups=mesh['row_0'=4,'row_1'=8,'z'=8,'core'=2] {'row_0','row_1'}, dimensions={0} | all-to-all | bytes 131072 | tf_op jit(solution)/shard_map/all_to_all | solution.py:40
  76.6 0.3 shard_map.59
  76.9 8.2 %all_gather.6 = f32[2,2,48,128]{3,2,1,0:T(8,128)S(1)} all-gather(f32[1,2,48,128]{3,2,1,0:T(8,128)S(1)} %bitcast.18), channel_id=1, replica_groups=mesh['row_0'=4,'row_1'=8,'z'=8,'core'=2] {'core'}, dimensions={0}, use_global_device_ids=true | all-gather | bytes 147456 | tf_op jit(solution)/shard_map/all_gather | solution.py:264
  85.1 20.1 %all_to_all.32 = f32[8,48,128]{2,1,0:T(8,128)S(1)} all-to-all(f32[8,48,128]{2,1,0:T(8,128)S(1)} %broadcast_in_dim.15), channel_id=1, replica_groups=mesh['row_0'=4,'row_1'=8,'z'=8,'core'=2] {'z'}, dimensions={0} | all-to-all | bytes 393216 | tf_op jit(solution)/shard_map/all_to_all | solution.py:40
  105.3 3.5 %all_gather.7.total = f32[96,128]{1,0:T(8,128)S(1)} all-gather(f32[48,128]{1,0:T(8,128)S(1)} %reduce_sum.38), channel_id=1, replica_groups=mesh['row_0'=4,'row_1'=8,'z'=8,'core'=2] {'core'}, dimensions={0}, use_global_device_ids=true | all-gather | bytes 73728 | tf_op jit(solution)/shard_map/all_gather | solution.py:267
  108.7 2.1 %shard_map.60 = (f32[64,128]{1,0:T(8,128)S(1)}, f32[8,32,128]{2,1,0:T(8,128)S(1)}) custom-call(f32[96,128]{1,0:T(8,128)S(1)} %all_gather.7.total), custom_call_target="tpu_custom_call" | custom-call | tf_op jit(solution)/shard_map/pallas_call | solution.py:213
  110.8 10.8 %all_to_all.33 = f32[8,32,128]{2,1,0:T(8,128)S(1)} all-to-all(f32[8,32,128]{2,1,0:T(8,128)S(1)} %get-tuple-element.16), channel_id=1, replica_groups=mesh['row_0'=4,'row_1'=8,'z'=8,'core'=2] {'row_1'}, dimensions={0} | all-to-all | bytes 262144 | tf_op jit(solution)/shard_map/all_to_all | solution.py:221
  121.6 6.8 %all_to_all.34.grams = f32[4,32,128]{2,1,0:T(8,128)S(1)} all-to-all(f32[4,32,128]{2,1,0:T(8,128)S(1)} %broadcast_in_dim.16), channel_id=1, replica_groups=mesh['row_0'=4,'row_1'=8,'z'=8,'core'=2] {'row_0'}, dimensions={0} | all-to-all | bytes 131072 | tf_op jit(solution)/shard_map/all_to_all | solution.py:40
  128.5 2.4 %shard_map.61 = f32[64,128]{1,0:T(8,128)} custom-call(f32[4,32,128]{2,1,0:T(8,128)S(1)} %all_to_all.34.grams, f32[64,128]{1,0:T(8,128)S(1)} %get-tuple-element.17.mapped), custom_call_target="tpu_custom_call" | custom-call | tf_op jit(solution)/shard_map/pallas_call | solution.py:213
  (13 shorter events, 0.2 us)
Async XLA Ops:
  0.6 0.8 copy-start.1
  0.7 0.7 copy-start.3
  1.5 15.8 %collective-permute-start.3 = (bf16[32,256]{1,0:T(8,128)(2,1)S(1)}, bf16[32,256]{1,0:T(8,128)(2,1)S(1)}, u32[]{:S(2)}, u32[]{:S(2)}) collective-permute-start(bf16[32,256]{1,0:T(8,128)(2,1)S(1)} %maximum_select_fusion), channel_id=1, source_target_pairs={{0,256},{1,287},{2,303},{3,304},{4,320},{5,351},{6,367},{7,368},{8... | collective-permute-start | bytes 49160 | tf_op jit(solution)/shard_map/ppermute | solution.py:254
  18.2 17.6 %copy-start.2 = (bf16[128,2,128]{2,1,0:T(2,128)(2,1)S(1)}, bf16[128,2,128]{2,1,0:T(2,128)(2,1)}, u32[]{:S(2)}) copy-start(bf16[128,2,128]{2,1,0:T(2,128)(2,1)} %param.5) | copy-start | bytes 196612
  18.2 24.1 %all-to-all-start = ((bf16[32,32,256]{2,1,0:T(8,128)(2,1)}), bf16[32,32,256]{2,1,0:T(8,128)(2,1)S(1)}, u32[]{:S(2)}, u32[]{:S(2)}) async-start(bf16[32,32,256]{2,1,0:T(8,128)(2,1)} %copies.1), calls=%async_computation | async-start | bytes 1048576 | tf_op jit(solution)/shard_map/all_to_all | solution.py:221
  25.5 12.1 %collective-permute-start = (bf16[128,256]{1,0:T(8,128)(2,1)S(1)}, bf16[128,256]{1,0:T(8,128)(2,1)S(1)}, u32[]{:S(2)}, u32[]{:S(2)}) collective-permute-start(bf16[128,256]{1,0:T(8,128)(2,1)S(1)} %bitcast.13), channel_id=1, source_target_pairs={{0,496},{16,0},{32,16},{48,32},{64,48},{80,64},{96,80},{112,96},{1... | collective-permute-start | bytes 196616 | tf_op jit(solution)/shard_map/ppermute | solution.py:255
  32.0 10.3 %collective-permute-start.1 = (bf16[128,256]{1,0:T(8,128)(2,1)S(1)}, bf16[128,256]{1,0:T(8,128)(2,1)S(1)}, u32[]{:S(2)}, u32[]{:S(2)}) collective-permute-start(bf16[128,256]{1,0:T(8,128)(2,1)S(1)} %bitcast.14), channel_id=1, source_target_pairs={{0,496},{16,480},{32,464},{48,448},{64,432},{80,416},{96,400},{112... | collective-permute-start | bytes 196616 | tf_op jit(solution)/shard_map/ppermute | solution.py:256
  35.1 7.2 %collective-permute-start.2 = (bf16[128,256]{1,0:T(8,128)(2,1)S(1)}, bf16[128,256]{1,0:T(8,128)(2,1)S(1)}, u32[]{:S(2)}, u32[]{:S(2)}) collective-permute-start(bf16[128,256]{1,0:T(8,128)(2,1)S(1)} %bitcast.15), channel_id=1, source_target_pairs={{0,0},{16,496},{32,480},{48,464},{64,448},{80,432},{96,416},{112,4... | collective-permute-start | bytes 196616 | tf_op jit(solution)/shard_map/ppermute | solution.py:257
  35.8 6.5 %copy-start = (f32[64,128]{1,0:T(8,128)S(1)}, f32[64,128]{1,0:T(8,128)}, u32[]{:S(2)}) copy-start(f32[64,128]{1,0:T(8,128)} %basis.1) | copy-start | bytes 98308
